TPU v7x, 16 devices: a 4x2x1 block of a 4x4x8 slice. The times are simulated.
16 devices in a mesh: rep: 2 (over y, z), dp: 8 (over x, core).
Axes of the slice: x: 4, y: 2, z: 1, core: 2. Of those that a mesh axis runs over, the one named last changes fastest.
The devices are a block of a 4x4x8 slice.
Arguments:
- x: bfloat16 [16, 2048, 512], P(('rep', 'dp')), parts along dimension 0
- dy: bfloat16 [16, 2048, 512], P(('rep', 'dp')), parts along dimension 0
- w_gate: bfloat16 [2, 512, 2048], replicated
- w_up: bfloat16 [2, 512, 2048], replicated
- w_down: bfloat16 [2, 2048, 512], replicated
- m_w_gate: float32 [2, 512, 2048], replicated
- m_w_up: float32 [2, 512, 2048], replicated
- m_w_down: float32 [2, 2048, 512], replicated
- v_w_gate: float32 [2, 512, 2048], replicated
- v_w_up: float32 [2, 512, 2048], replicated
- v_w_down: float32 [2, 2048, 512], replicated
Outputs:
- output 1: bfloat16 [4, 512, 2048], P('rep'), parts along dimension 0
- output 2: bfloat16 [4, 512, 2048], P('rep'), parts along dimension 0
- output 3: bfloat16 [4, 2048, 512], P('rep'), parts along dimension 0
- output 4: float32 [4, 512, 2048], P('rep'), parts along dimension 0
- output 5: float32 [4, 512, 2048], P('rep'), parts along dimension 0
- output 6: float32 [4, 2048, 512], P('rep'), parts along dimension 0
- output 7: float32 [4, 512, 2048], P('rep'), parts along dimension 0
- output 8: float32 [4, 512, 2048], P('rep'), parts along dimension 0
- output 9: float32 [4, 2048, 512], P('rep'), parts along dimension 0
There are 2 independent parts. A program takes and returns all parts, laid end to end along the dimension named above; an argument that names none is the same for every part.
All inputs are finite; a program needn't handle non-finite values.
Results may differ from a plain program's by a relative error of at most 0.022.
Values are sent between devices in bfloat16 or wider.
A program may use at most 768 MiB of HBM per device.

v0:
```python
import jax
import jax.numpy as jnp
from jax import lax
from jax.sharding import PartitionSpec as P

NAMES = ("w_gate", "w_up", "w_down")


def matmul(a, w):
    return jnp.dot(a, w, preferred_element_type=jnp.float32).astype(jnp.bfloat16)


def normed(h):
    wide = h.astype(jnp.float32)
    scale = lax.rsqrt(jnp.mean(wide**2, -1, keepdims=True) + 1e-6)
    return (wide * scale).astype(jnp.bfloat16)


def layer(h, w):
    a = normed(h)
    gate = jnp.dot(a, w["w_gate"], preferred_element_type=jnp.float32)
    up = jnp.dot(a, w["w_up"], preferred_element_type=jnp.float32)
    return h + matmul((jax.nn.silu(gate) * up).astype(jnp.bfloat16), w["w_down"])


def adamw(w, m, v, g):
    m = 0.9 * m + 0.1 * g
    v = 0.95 * v + 0.05 * g * g
    step = m * lax.rsqrt(v + 1e-8) + 0.1 * w
    return (w - 0.02 * step).astype(jnp.bfloat16), m, v


def clipped(gradients, sum_of_squares, count):
    factor = jnp.minimum(1.0, 0.5 * lax.rsqrt(sum_of_squares / count + 1e-30))
    return [g * factor for g in gradients]


def solution(mesh):
    def step(x, dy, *arrays):
        weights, m, v = (arrays[i : i + 3] for i in (0, 3, 6))
        layers = weights[0].shape[0]
        h, kept = x[0], []
        for number in range(layers):
            kept.append(h)
            h = layer(h, {name: w[number] for name, w in zip(NAMES, weights, strict=True)})
        by_h, summed = dy[0], [None] * layers
        for number in reversed(range(layers)):
            _, back = jax.vjp(lambda w, h: layer(h, w), {name: w[number] for name, w in zip(NAMES, weights, strict=True)}, kept[number])
            by_w, by_h = back(by_h)
            summed[number] = [lax.psum(by_w[name], "dp") for name in NAMES]
        gradients = [jnp.stack([summed[number][i] for number in range(layers)]).astype(jnp.float32) for i in range(3)]
        gradients = clipped(gradients, sum(jnp.sum(g * g) for g in gradients), sum(g.size for g in gradients))
        new = [adamw(w.astype(jnp.float32), m, v, g) for w, m, v, g in zip(weights, m, v, gradients, strict=True)]
        return tuple(one[which] for which in range(3) for one in new)

    return jax.shard_map(
        step,
        mesh=mesh,
        in_specs=(P(("rep", "dp"), None, None),) * 2 + (P(None, None, None),) * 9,
        out_specs=(P("rep", None, None),) * 9,
        check_vma=False,
    )
```

profile of v0, /device:TPU:113, one launch (start us, length us, event | category | flops | bytes accessed | tf_op | source)
XLA Modules:
  0.0 399.1 jit_solution(10278326371045639322)
XLA Ops:
  7.3 2.9 copy.20
  10.7 4.2 %copy.21 = bf16[1,2048,512]{1,2,0:T(8,128)(2,1)} copy(bf16[1,2048,512]{2,1,0:T(8,128)(2,1)} %param.12) | data formatting | bytes 4194304 | tf_op args[1]
  14.9 10.3 %convolution_convert_fusion.1 = bf16[2048,2048]{1,0:T(8,128)(2,1)} fusion(bf16[1,2048,512]{2,1,0:T(8,128)(2,1)} %param.12, bf16[2,2048,512]{2,1,0:T(8,128)(2,1)} %param.15), kind=kOutput, calls=%fused_computation.61 | convolution fusion | flops 4299161600 | bytes 12582912 | tf_op jit(solution)/shard_map/transpose(jvp())/dot_general | solution.py:10
  25.2 8.2 %fusion.76 = f32[2048,2048]{1,0:T(8,128)} fusion(bf16[2,512,2048]{2,1,0:T(8,128)(2,1)S(1)} %copy-done.9, bf16[1,2048,512]{2,1,0:T(8,128)(2,1)S(1)} %copy-done.13, f32[2048]{0:T(1024)S(1)} %add_rsqrt_fusion), kind=kOutput, calls=%fused_computation.112 | convolution fusion | flops 4298113024 | bytes 20979712 | tf_op jit(solution)/shard_map/dot_general | solution.py:21
  33.4 17.4 %multiply_convert_fusion.1 = (bf16[2048,2048]{1,0:T(8,128)(2,1)}, f32[2048,2048]{1,0:T(8,128)}) fusion(f32[2048,2048]{1,0:T(8,128)} %fusion.76, bf16[2,512,2048]{2,1,0:T(8,128)(2,1)} %param.14, bf16[1,2048,512]{2,1,0:T(8,128)(2,1)S(1)} %copy-done.13, f32[2048]{0:T(1024)S(1)} %add_rsqrt_fusion), kind=kOutput, calls=%fused_computation.17 | convolution fusion | flops 4323278848 | bytes 46145536 | tf_op jit(solution)/shard_map/dot_general | solution.py:22
  50.8 9.1 %fusion.40 = (f32[2048]{0:T(1024)S(1)}, bf16[2048,512]{0,1:T(8,128)(2,1)S(1)}) fusion(bf16[2048,2048]{1,0:T(8,128)(2,1)} %get-tuple-element.24, bf16[2,2048,512]{2,1,0:T(8,128)(2,1)} %param.15, bf16[1,2048,512]{1,2,0:T(8,128)(2,1)S(1)} %copy.20), kind=kOutput, calls=%fused_computation.73 | convolution fusion | flops 4300208128 | bytes 14688256 | tf_op jit(solution)/shard_map/dot_general | solution.py:10
  61.2 8.2 %fusion.65 = f32[2048,2048]{1,0:T(8,128)} fusion(bf16[2,512,2048]{2,1,0:T(8,128)(2,1)S(1)} %copy-done.11, bf16[2048,512]{0,1:T(8,128)(2,1)S(1)} %get-tuple-element.27, f32[2048]{0:T(1024)S(1)} %fusion.95), kind=kOutput, calls=%fused_computation.101 | convolution fusion | flops 4298113024 | bytes 20979712 | tf_op jit(solution)/shard_map/jvp()/dot_general | solution.py:22
  69.5 23.2 %fusion.2 = (bf16[2048,2048]{1,0:T(8,128)(2,1)}, f32[2048,2048]{1,0:T(8,128)}) fusion(f32[2048,2048]{1,0:T(8,128)} %fusion.65, bf16[2048,2048]{1,0:T(8,128)(2,1)} %convolution_convert_fusion.1, bf16[2,512,2048]{2,1,0:T(8,128)(2,1)} %param.13, bf16[2048,512]{0,1:T(8,128)(2,1)} %copy-done.15, f32[2048]{0:T(1024)S(1)} %fusion.95), kind=kOutput, calls=%fused_computation.8 | convolution fusion | flops 4348444672 | bytes 54534144 | tf_op jit(solution)/shard_map/jvp()/dot_general | solution.py:21
  92.7 14.5 %fusion.55 = bf16[1,2048,512]{2,1,0:T(8,128)(2,1)} fusion(f32[2048,2048]{1,0:T(8,128)} %fusion.65, bf16[1,2048,512]{2,1,0:T(8,128)(2,1)S(1)} %copy-done.14, f32[2048,2048]{1,0:T(8,128)} %get-tuple-element.29), kind=kOutput, calls=%fused_computation.93 | convolution fusion | flops 4321181696 | bytes 37748736 | tf_op jit(solution)/shard_map/transpose(jvp())/dot_general | solution.py:10
  107.2 12.4 %fusion.54 = bf16[1,512,2048]{2,1,0:T(8,128)(2,1)} fusion(bf16[2048,2048]{1,0:T(8,128)(2,1)} %convolution_convert_fusion.1, bf16[2048,512]{0,1:T(8,128)(2,1)S(1)} %copy-done.16, f32[2048]{0:T(1024)S(1)} %fusion.95, f32[2048,2048]{1,0:T(8,128)} %get-tuple-element.29), kind=kOutput, calls=%fused_computation.92 | convolution fusion | flops 4324327424 | bytes 29368320 | tf_op jit(solution)/shard_map/transpose(jvp())/dot_general | solution.py:22
  119.6 11.3 %fusion.47 = bf16[2048,512]{0,1:T(8,128)(2,1)S(1)} fusion(bf16[2048,2048]{1,0:T(8,128)(2,1)} %convolution_convert_fusion.1, bf16[2,512,2048]{2,1,0:T(8,128)(2,1)S(1)} %copy-done.12, f32[2048,2048]{1,0:T(8,128)} %get-tuple-element.29), kind=kOutput, calls=%fused_computation.84 | convolution fusion | flops 4321181696 | bytes 29360128 | tf_op jit(solution)/shard_map/transpose(jvp())/dot_general | solution.py:22
  130.9 9.3 %fusion.52 = bf16[1,512,2048]{2,1,0:T(8,128)(2,1)} fusion(bf16[2048,2048]{1,0:T(8,128)(2,1)} %get-tuple-element.28, bf16[2048,512]{0,1:T(8,128)(2,1)S(1)} %copy-done.16, f32[2048]{0:T(1024)S(1)} %fusion.95), kind=kOutput, calls=%fused_computation.90 | convolution fusion | flops 4298113024 | bytes 12591104 | tf_op jit(solution)/shard_map/transpose(jvp())/dot_general | solution.py:21
  140.2 9.0 %fusion.42 = (f32[2048]{0:T(1024)S(1)}, bf16[2048,512]{0,1:T(8,128)(2,1)S(1)}) fusion(bf16[2048,512]{0,1:T(8,128)(2,1)S(1)} %copy-done.16, bf16[2048,512]{0,1:T(8,128)(2,1)S(1)} %fusion.47, bf16[2048,2048]{1,0:T(8,128)(2,1)} %get-tuple-element.28, bf16[2,512,2048]{2,1,0:T(8,128)(2,1)S(1)} %copy-done.10), kind=kOutput, calls=%fused_computation.75 | convolution fusion | flops 4300208128 | bytes 16785408 | tf_op jit(solution)/shard_map/transpose(jvp())/dot_general | solution.py:21
  149.2 1.4 fusion.62
  150.7 9.7 %fusion.51 = bf16[1,2048,512]{2,1,0:T(8,128)(2,1)} fusion(bf16[2048,2048]{1,0:T(8,128)(2,1)} %get-tuple-element.24, bf16[2048,512]{0,1:T(8,128)(2,1)S(1)} %fusion.62), kind=kOutput, calls=%fused_computation.89 | convolution fusion | flops 4296015872 | bytes 12582912 | tf_op jit(solution)/shard_map/transpose(jvp())/dot_general | solution.py:10
  160.3 5.1 %convolution_convert_fusion = bf16[2048,2048]{1,0:T(8,128)(2,1)S(1)} fusion(bf16[2048,512]{0,1:T(8,128)(2,1)S(1)} %fusion.62, bf16[2,2048,512]{2,1,0:T(8,128)(2,1)S(1)} %copy-done.8), kind=kOutput, calls=%fused_computation.60 | convolution fusion | flops 4299161600 | bytes 12582912 | tf_op jit(solution)/shard_map/transpose(jvp())/dot_general | solution.py:10
  165.5 13.5 %fusion.53 = bf16[1,512,2048]{2,1,0:T(8,128)(2,1)} fusion(bf16[2048,2048]{1,0:T(8,128)(2,1)S(1)} %convolution_convert_fusion, f32[2048,2048]{1,0:T(8,128)} %fusion.76, bf16[1,2048,512]{1,2,0:T(8,128)(2,1)S(1)} %copy-done.6, f32[2048]{0:T(1024)S(1)} %copy-done.20), kind=kOutput, calls=%fused_computation.91 | convolution fusion | flops 4324327424 | bytes 29368320 | tf_op jit(solution)/shard_map/transpose(jvp())/dot_general | solution.py:22
  179.0 17.6 %fusion.56 = bf16[1,512,2048]{2,1,0:T(8,128)(2,1)} fusion(f32[2048,2048]{1,0:T(8,128)} %fusion.76, f32[2048,2048]{1,0:T(8,128)} %get-tuple-element.25, bf16[2048,2048]{1,0:T(8,128)(2,1)} %copy-done.21, bf16[1,2048,512]{1,2,0:T(8,128)(2,1)S(1)} %copy-done.6, f32[2048]{0:T(1024)S(1)} %copy-done.20), kind=kOutput, calls=%fused_computation.94 | convolution fusion | flops 4345298944 | bytes 46145536 | tf_op jit(solution)/shard_map/transpose(jvp())/dot_general | solution.py:21
  196.6 138.4 %all-reduce.3.cloned.1.call-done = (bf16[1,512,2048]{2,1,0:T(8,128)(2,1)}, bf16[1,512,2048]{2,1,0:T(8,128)(2,1)}, bf16[1,512,2048]{2,1,0:T(8,128)(2,1)}, bf16[1,...) async-done(((bf16[1,512,2048]{2,1,0:T(8,128)(2,1)}, bf16[1,512,2048]{2,1,0:T(8,128)(2,1)}, bf16[1,512,2048]{2,1,0:T(8,128)(2,1)}, ...) | async-done | bytes 12582928 | tf_op jit(solution)/shard_map/psum | solution.py:50
  335.1 4.5 %fusion.24 = f32[]{:T(128)} fusion(bf16[1,2048,512]{2,1,0:T(8,128)(2,1)} %get-tuple-element.13, bf16[1,2048,512]{2,1,0:T(8,128)(2,1)} %get-tuple-element.14), kind=kLoop, calls=%fused_computation.48 | loop fusion | flops 8388607 | bytes 4194308 | tf_op jit(solution)/shard_map/reduce_sum | solution.py:52
  339.5 4.3 %fusion.23 = f32[]{:T(128)} fusion(bf16[1,512,2048]{2,1,0:T(8,128)(2,1)} %get-tuple-element.11, bf16[1,512,2048]{2,1,0:T(8,128)(2,1)} %get-tuple-element.12), kind=kLoop, calls=%fused_computation.47 | loop fusion | flops 8388607 | bytes 4194308 | tf_op jit(solution)/shard_map/reduce_sum | solution.py:52
  343.8 2.8 fusion.22
  348.6 15.8 %fusion.30 = (bf16[2,2048,512]{2,1,0:T(8,128)(2,1)}, f32[2,2048,512]{2,1,0:T(8,128)}, f32[2,2048,512]{2,1,0:T(8,128)}) fusion(bf16[2,2048,512]{2,1,0:T(8,128)(2,1)} %param.15, f32[]{:T(128)S(6)} %min_shard_map.3, bf16[1,2048,512]{2,1,0:T(8,128)(2,1)} %get-tuple-element.13, bf16[1,2048,512]{2,1,0:T(8,128)(2,1)} %get-tuple-element.14, ...), kind=kLoop, calls=%fused_computation.54 | loop fusion | flops 41943040 | bytes 46137348 | tf_op jit(solution)/shard_map/convert_element_type | solution.py:30
  364.5 27.4 %fusion.21 = (bf16[2,512,2048]{2,1,0:T(8,128)(2,1)}, f32[2,512,2048]{2,1,0:T(8,128)}, f32[2,512,2048]{2,1,0:T(8,128)}, bf16[2,512,2048]{2,1,0:T(8,128)(2,1)}, f3...) fusion(bf16[2,512,2048]{2,1,0:T(8,128)(2,1)} %param.13, f32[]{:T(128)S(6)} %min_shard_map.3, ...), kind=kLoop, calls=%fused_computation.45 | loop fusion | flops 83886080 | bytes 92274688 | tf_op jit(solution)/shard_map/convert_element_type | solution.py:30
  (50 shorter events, 2.0 us)
Async XLA Ops:
  7.2 327.9 %all-reduce.3.cloned.1.call-start = ((), (), s32[]{:S(2)}) async-start(), calls=%async_computation | async-start | bytes 25165824 | tf_op jit(solution)/shard_map/psum | solution.py:50
  10.2 40.6 %copy-start.5 = (bf16[1,2048,512]{1,2,0:T(8,128)(2,1)}, bf16[1,2048,512]{1,2,0:T(8,128)(2,1)S(1)}, u32[]{:S(2)}) copy-start(bf16[1,2048,512]{1,2,0:T(8,128)(2,1)S(1)} %copy.20) | copy-start | bytes 6291460
  10.7 22.7 %copy-start.19 = (f32[2048]{0:T(1024)}, f32[2048]{0:T(1024)S(1)}, u32[]{:S(2)}) copy-start(f32[2048]{0:T(1024)S(1)} %add_rsqrt_fusion) | copy-start | bytes 24580
  14.8 10.3 %copy-start.9 = (bf16[2,512,2048]{2,1,0:T(8,128)(2,1)S(1)}, bf16[2,512,2048]{2,1,0:T(8,128)(2,1)}, u32[]{:S(2)}) copy-start(bf16[2,512,2048]{2,1,0:T(8,128)(2,1)} %param.13) | copy-start | bytes 12582916
  14.8 10.3 %copy-start.13 = (bf16[1,2048,512]{2,1,0:T(8,128)(2,1)S(1)}, bf16[1,2048,512]{2,1,0:T(8,128)(2,1)}, u32[]{:S(2)}) copy-start(bf16[1,2048,512]{2,1,0:T(8,128)(2,1)} %param.11) | copy-start | bytes 6291460
  50.8 10.4 %copy-start.11 = (bf16[2,512,2048]{2,1,0:T(8,128)(2,1)S(1)}, bf16[2,512,2048]{2,1,0:T(8,128)(2,1)}, u32[]{:S(2)}) copy-start(bf16[2,512,2048]{2,1,0:T(8,128)(2,1)} %param.14) | copy-start | bytes 12582916
  59.9 1.3 copy-start.15
  59.9 1.3 copy-start.17
  69.5 23.3 %copy-start.14 = (bf16[1,2048,512]{2,1,0:T(8,128)(2,1)S(1)}, bf16[1,2048,512]{2,1,0:T(8,128)(2,1)}, u32[]{:S(2)}) copy-start(bf16[1,2048,512]{2,1,0:T(8,128)(2,1)} %param.12) | copy-start | bytes 6291460
  92.7 14.5 %copy-start.16 = (bf16[2048,512]{0,1:T(8,128)(2,1)S(1)}, bf16[2048,512]{0,1:T(8,128)(2,1)}, u32[]{:S(2)}) copy-start(bf16[2048,512]{0,1:T(8,128)(2,1)} %copy-done.15) | copy-start | bytes 6291460
  107.2 12.4 %copy-start.12 = (bf16[2,512,2048]{2,1,0:T(8,128)(2,1)S(1)}, bf16[2,512,2048]{2,1,0:T(8,128)(2,1)}, u32[]{:S(2)}) copy-start(bf16[2,512,2048]{2,1,0:T(8,128)(2,1)} %param.14) | copy-start | bytes 12582916
  130.9 9.3 %copy-start.10 = (bf16[2,512,2048]{2,1,0:T(8,128)(2,1)S(1)}, bf16[2,512,2048]{2,1,0:T(8,128)(2,1)}, u32[]{:S(2)}) copy-start(bf16[2,512,2048]{2,1,0:T(8,128)(2,1)} %param.13) | copy-start | bytes 12582916
  140.2 9.0 %copy-start.18 = (f32[2048]{0:T(1024)S(1)}, f32[2048]{0:T(1024)}, u32[]{:S(2)}) copy-start(f32[2048]{0:T(1024)} %copy-done.17) | copy-start | bytes 24580
  140.2 9.1 %copy-start.7 = (bf16[1,2048,512]{1,2,0:T(8,128)(2,1)S(1)}, bf16[1,2048,512]{1,2,0:T(8,128)(2,1)}, u32[]{:S(2)}) copy-start(bf16[1,2048,512]{1,2,0:T(8,128)(2,1)} %copy.21) | copy-start | bytes 6291460
  150.6 9.7 %copy-start.8 = (bf16[2,2048,512]{2,1,0:T(8,128)(2,1)S(1)}, bf16[2,2048,512]{2,1,0:T(8,128)(2,1)}, u32[]{:S(2)}) copy-start(bf16[2,2048,512]{2,1,0:T(8,128)(2,1)} %param.15) | copy-start | bytes 12582916
  160.3 5.1 %copy-start.6 = (bf16[1,2048,512]{1,2,0:T(8,128)(2,1)S(1)}, bf16[1,2048,512]{1,2,0:T(8,128)(2,1)}, u32[]{:S(2)}) copy-start(bf16[1,2048,512]{1,2,0:T(8,128)(2,1)} %copy-done.5) | copy-start | bytes 6291460
  160.3 5.1 %copy-start.20 = (f32[2048]{0:T(1024)S(1)}, f32[2048]{0:T(1024)}, u32[]{:S(2)}) copy-start(f32[2048]{0:T(1024)} %copy-done.19) | copy-start | bytes 24580
  165.5 13.5 %copy-start.21 = (bf16[2048,2048]{1,0:T(8,128)(2,1)}, bf16[2048,2048]{1,0:T(8,128)(2,1)S(1)}, u32[]{:S(2)}) copy-start(bf16[2048,2048]{1,0:T(8,128)(2,1)S(1)} %convolution_convert_fusion) | copy-start | bytes 25165828
  335.1 8.8 %copy-start = (bf16[1,512,2048]{2,1,0:T(8,128)(2,1)S(1)}, bf16[1,512,2048]{2,1,0:T(8,128)(2,1)}, u32[]{:S(2)}) copy-start(bf16[1,512,2048]{2,1,0:T(8,128)(2,1)} %get-tuple-element.9) | copy-start | bytes 6291460
  335.1 8.8 %copy-start.1 = (bf16[1,512,2048]{2,1,0:T(8,128)(2,1)S(1)}, bf16[1,512,2048]{2,1,0:T(8,128)(2,1)}, u32[]{:S(2)}) copy-start(bf16[1,512,2048]{2,1,0:T(8,128)(2,1)} %get-tuple-element.10) | copy-start | bytes 6291460
  348.6 15.9 %copy-start.2 = (bf16[1,512,2048]{2,1,0:T(8,128)(2,1)S(1)}, bf16[1,512,2048]{2,1,0:T(8,128)(2,1)}, u32[]{:S(2)}) copy-start(bf16[1,512,2048]{2,1,0:T(8,128)(2,1)} %get-tuple-element.10) | copy-start | bytes 6291460
  348.6 15.9 %copy-start.3 = (bf16[1,512,2048]{2,1,0:T(8,128)(2,1)S(1)}, bf16[1,512,2048]{2,1,0:T(8,128)(2,1)}, u32[]{:S(2)}) copy-start(bf16[1,512,2048]{2,1,0:T(8,128)(2,1)} %get-tuple-element.11) | copy-start | bytes 6291460
  348.6 15.9 %copy-start.4 = (bf16[1,512,2048]{2,1,0:T(8,128)(2,1)S(1)}, bf16[1,512,2048]{2,1,0:T(8,128)(2,1)}, u32[]{:S(2)}) copy-start(bf16[1,512,2048]{2,1,0:T(8,128)(2,1)} %get-tuple-element.12) | copy-start | bytes 6291460
Sparse Core Ops, SparseCore 0:
  196.7 138.2 all-reduce.2
where the time goes:
time: 407 us; the launch traced here: 399 us
  matrix products  179 us (44%)
  waiting for transfers between devices  138 us (34%)
  other arithmetic  56.6 us (14%)
  between operations  16.7 us (4%)
  local copies, waits for them, and re-layouts  8.48 us (2%)
    psum x1, waiting for transfers between devices, step(): summed[number] = [lax.psum(by_w[name], 'dp') for name in NAMES]  138 us
    dot_general x5, matrix products, layer(): gate = jnp.dot(a, w['w_gate'], preferred_element_type=jnp.float32)  67.3 us
    dot_general x5, matrix products, layer(): up = jnp.dot(a, w['w_up'], preferred_element_type=jnp.float32)  62.8 us
    dot_general x5, matrix products, matmul(): jnp.dot(a, w, preferred_element_type=jnp.float32).astype(jnp.bfloat16)  48.6 us
    convert_element_type x2, other arithmetic, adamw(): return ((w - 0.02 * step).astype(jnp.bfloat16), m, v)  43.2 us
    reduce_sum x3, other arithmetic, step(): jnp.sum(g * g)  11.5 us
    unnamed x46, local copies, waits for them, and re-layouts  8.48 us
  transfers between devices with their start and end apart: 1, of which 1 were waited for; matrix products, arithmetic and copies ran while one was open for 0% of the time, Pallas kernels for 0%

commit v1 on v0

v1 whole, which is shorter than its diff:
```python
import functools

import jax
import jax.numpy as jnp
from jax import lax
from jax.experimental import pallas as pl
from jax.experimental.pallas import tpu as pltpu
from jax.sharding import PartitionSpec as P

MESH = pl.DeviceIdType.MESH
BF16, F32 = jnp.bfloat16, jnp.float32
CORES = 2
CHUNK = 256
TILE = 512
FTILE = 256
SLOTS = 4
TERMS = 5
HALVES = 7
RUNS = 6
COMM = True


def dot(a, b):
    return jnp.dot(a, b, preferred_element_type=F32)


def dot_t(a, b):
    return lax.dot_general(a, b, (((1,), (1,)), ((), ())), preferred_element_type=F32)


def sigmoid(z):
    return 0.5 * jnp.tanh(0.5 * z) + 0.5


def norm_scale(wide):
    return lax.rsqrt(jnp.mean(wide * wide, -1, keepdims=True) + 1e-6)


def grad_kernel(
    dp, layers, x_hbm, dy_hbm, wg_hbm, wu_hbm, wd_hbm, g_hbm, ssq_out,
    xv, dyv, hv, av, at, dt, acc, actf, act, dgu, wgu, wd, term, from_core, run, g, ssq, ssq_all,
    io_sem, w_sem, out_sem, core_sem, ring_send, ring_recv, near_send, near_recv, far_send, far_recv, half_sem, ssq_send, ssq_recv,
):
    tokens, d = xv.shape
    ff = wd_hbm.shape[1]
    per = ff // CHUNK
    total = layers * per
    chips = dp // CORES
    rows = g.shape[1]
    half = rows // CORES
    own = half // chips
    piece = own // 2
    rep = lax.axis_index("rep")
    me = lax.axis_index("dp")
    chip, core = me // CORES, me % CORES
    other = 1 - core

    def device(chip, core):
        return (rep, chip * CORES + core)

    right, left = device((chip + 1) % chips, core), device((chip + chips - 1) % chips, core)
    sibling = device(chip, other)

    barrier = pltpu.get_barrier_semaphore()
    if COMM:
        for k in range(1, dp):
            pl.semaphore_signal(barrier, inc=1, device_id=(rep, (me + k) % dp), device_id_type=MESH)

    def load_x():
        return pltpu.make_async_copy(x_hbm, xv, io_sem.at[0])

    def load_dy():
        return pltpu.make_async_copy(dy_hbm, dyv, io_sem.at[1])

    def load_w(layer):
        copies = []
        for c in range(per):
            cut = slice(c * CHUNK, (c + 1) * CHUNK)
            copies.append(pltpu.make_async_copy(wg_hbm.at[layer, :, cut], wgu.at[layer, c, :, :CHUNK], w_sem.at[layer, c, 0]))
            copies.append(pltpu.make_async_copy(wu_hbm.at[layer, :, cut], wgu.at[layer, c, :, CHUNK:], w_sem.at[layer, c, 1]))
            copies.append(pltpu.make_async_copy(wd_hbm.at[layer, cut, :], wd.at[layer, cut, :], w_sem.at[layer, c, 2]))
        return copies

    load_x().start()
    for copy in load_w(0):
        copy.start()
    load_dy().start()
    for copy in load_w(1):
        copy.start()

    load_x().wait()
    for copy in load_w(0):
        copy.wait()
    load_dy().wait()

    @pl.loop(0, tokens // FTILE)
    def _(t):
        at_t = pl.ds(pl.multiple_of(t * FTILE, FTILE), FTILE)
        wide = xv[at_t, :].astype(F32)
        a = (wide * norm_scale(wide)).astype(BF16)
        for c in range(per):
            gu = dot(a, wgu[0, c])
            gate, up = gu[:, :CHUNK], gu[:, CHUNK:]
            actf[:, c * CHUNK : (c + 1) * CHUNK] = (gate * sigmoid(gate) * up).astype(BF16)
        h = xv[at_t, :] + dot(actf[...], wd[0]).astype(BF16)
        hv[at_t, :] = h
        wide = h.astype(F32)
        a = (wide * norm_scale(wide)).astype(BF16)
        av[at_t, :] = a
        at[:, at_t] = a.T
        dt[:, at_t] = dyv[at_t, :].T

    for copy in load_w(1):
        copy.wait()

    def compute(layer, c, i):
        w_chunk = wgu[layer, c]
        d_chunk = wd[layer, pl.ds(pl.multiple_of(c * CHUNK, CHUNK), CHUNK), :]
        for t in range(tokens // TILE):
            at_t = slice(t * TILE, (t + 1) * TILE)
            gu = dot(av[at_t, :], w_chunk)
            by_act = dot_t(dyv[at_t, :], d_chunk).astype(BF16).astype(F32)
            gate, up = gu[:, :CHUNK], gu[:, CHUNK:]
            s = sigmoid(gate)
            silu = gate * s
            act[at_t, :] = (silu * up).astype(BF16)
            dgu[at_t, :CHUNK] = (by_act * up * (s + silu * (1.0 - s))).astype(BF16)
            dgu[at_t, CHUNK:] = (by_act * silu).astype(BF16)
            if layer > 0:
                by_a = dot_t(dgu[at_t, :], w_chunk)
                acc[at_t, :] += by_a
        slot = i % TERMS
        by_gu = dot(at[...], dgu[...]).astype(BF16)
        term[slot, 0:d, :] = by_gu[:, :CHUNK]
        term[slot, d : 2 * d, :] = by_gu[:, CHUNK:]
        by_d = dot(dt[...], act[...]).T.astype(BF16)
        for n in range(d // CHUNK):
            term[slot, 2 * d + n * CHUNK : 2 * d + (n + 1) * CHUNK, :] = by_d[:, n * CHUNK : (n + 1) * CHUNK]

    def remote(src, dst, send, recv, to):
        return pltpu.make_async_remote_copy(src_ref=src, dst_ref=dst, send_sem=send, recv_sem=recv, device_id=to, device_id_type=MESH)

    def rows_at(core, chip, direction=0, count=None):
        start = core * half + chip * own + direction * piece
        return pl.ds(pl.multiple_of(start, piece), piece if count is None else count)

    def swap(j):
        there = pl.ds(pl.multiple_of(other * half, half), half)
        return remote(term.at[j % TERMS, there], from_core.at[j % HALVES], core_sem.at[0, j % SLOTS], core_sem.at[1, j % SLOTS], sibling)

    def ring(j, step, direction):
        src, dst = (run.at[j % RUNS, n, direction] for n in (step - 1, step))
        sems = (step - 1, direction, j % SLOTS)
        return remote(src, dst, ring_send.at[sems], ring_recv.at[sems], right if direction == 0 else left)

    def near(j, direction, arriving=False):
        if arriving:
            block = (chip + chips - 1) % chips if direction == 0 else (chip + 1) % chips
        else:
            block = chip
        place = g.at[j, rows_at(core, block, 0, own)]
        return remote(place, place, near_send.at[direction, j], near_recv.at[direction, j], right if direction == 0 else left)

    def far(j, direction, arriving=False):
        if arriving:
            block = (chip + 2) % chips
        else:
            block = (chip + chips - 1) % chips if direction == 0 else (chip + 1) % chips
        place = g.at[j, rows_at(core, block, direction)]
        return remote(place, place, far_send.at[direction, j], far_recv.at[direction, j], right if direction == 0 else left)

    def share(j, arriving=False):
        place = g.at[j, pl.ds(pl.multiple_of((other if arriving else core) * half, half), half)]
        return remote(place, place, half_sem.at[0, j], half_sem.at[1, j], sibling)

    def put_out(j):
        return pltpu.make_async_copy(g.at[j], g_hbm.at[pl.ds(pl.multiple_of(j * rows, rows), rows)], out_sem.at[j % SLOTS])

    def add_up(j, p, direction):
        block = (chip + 2 * chips - p) % chips if direction == 0 else (chip + p) % chips
        here = rows_at(core, block, direction)
        within = pl.ds(pl.multiple_of(block * own + direction * piece, piece), piece)
        value = term[j % TERMS, here, :].astype(F32) + from_core[j % HALVES, within, :].astype(F32)
        if p > 1:
            value = value + run[j % RUNS, p - 1, direction].astype(F32)
        value = value.astype(BF16)
        if p < chips:
            run[j % RUNS, p - 1, direction] = value
        else:
            g[j, here, :] = value
        return value

    def phases(i):
        def at_chunk(j, body):
            pl.when((j >= 0) & (j < total))(functools.partial(body, j))

        def start_swap(j):
            swap(j).start()

        def ring_phase(p, j):
            if p == 1:
                swap(j).wait()
            for direction in range(2):
                if p > 1:
                    ring(j, p - 1, direction).wait()
                value = add_up(j, p, direction)
                if p < chips:
                    ring(j, p, direction).start()
                else:
                    wide = value.astype(F32)
                    wide = jnp.sum((wide * wide).reshape(piece // 8, 8, CHUNK), 0)
                    ssq[...] += sum(wide[:, n : n + 128] for n in range(0, CHUNK, 128))
            if p == chips:
                near(j, 0).start()
                near(j, 1).start()

        def far_phase(j):
            for direction in range(2):
                near(j, direction).wait_send()
                near(j, direction, True).wait_recv()
                far(j, direction).start()

        def share_phase(j):
            for direction in range(2):
                far(j, direction).wait_send()
                far(j, direction, True).wait_recv()
            share(j).start()

        def out_phase(j):
            share(j).wait_send()
            share(j, True).wait_recv()
            put_out(j).start()

        at_chunk(i, start_swap)
        for p in range(1, chips + 1):
            at_chunk(i - p, functools.partial(ring_phase, p))
        at_chunk(i - chips - 1, far_phase)
        at_chunk(i - chips - 2, share_phase)
        at_chunk(i - chips - 3, out_phase)
        at_chunk(i - chips - 4, lambda j: put_out(j).wait())

    acc[...] = jnp.zeros_like(acc)
    ssq[...] = jnp.zeros_like(ssq)
    if COMM:
        pl.semaphore_wait(barrier, dp - 1)

    @pl.loop(0, per)
    def _(c):
        compute(1, c, c)
        if COMM:
            phases(c)

    @pl.loop(0, tokens // FTILE)
    def _(t):
        at_t = pl.ds(pl.multiple_of(t * FTILE, FTILE), FTILE)
        wide = hv[at_t, :].astype(F32)
        scale = norm_scale(wide)
        by_a = acc[at_t, :].astype(BF16).astype(F32)
        by_h = by_a * scale - wide * (scale * scale * scale * jnp.mean(by_a * wide, -1, keepdims=True))
        by_h = dyv[at_t, :] + by_h.astype(BF16)
        dyv[at_t, :] = by_h
        dt[:, at_t] = by_h.T
        wide = xv[at_t, :].astype(F32)
        a = (wide * norm_scale(wide)).astype(BF16)
        av[at_t, :] = a
        at[:, at_t] = a.T

    @pl.loop(0, per)
    def _(c):
        compute(0, c, c + per)
        if COMM:
            phases(c + per)

    if COMM:
        def to_peer(k):
            peer = (me + k) % dp
            return remote(ssq, ssq_all.at[me], ssq_send.at[k - 1], ssq_recv.at[k - 1], (rep, peer))

        def from_peer(k):
            peer = (me + dp - k) % dp
            return remote(ssq, ssq_all.at[peer], ssq_send.at[k - 1], ssq_recv.at[k - 1], (rep, peer))

        @pl.loop(total, total + chips + 1)
        def _(i):
            phases(i)

        for k in range(1, dp):
            to_peer(k).start()
        ssq_all[me] = ssq[...]

        @pl.loop(total + chips + 1, total + chips + 5)
        def _(i):
            phases(i)

        for k in range(1, dp):
            to_peer(k).wait_send()
            from_peer(k).wait_recv()
        ssq_out[...] = ssq_all[...]
    else:
        ssq_out[...] = jnp.zeros_like(ssq_out)


def gradients(x, dy, wg, wu, wd, dp):
    tokens, d = x.shape
    layers, _, ff = wg.shape
    per = ff // CHUNK
    total = layers * per
    rows = 3 * d * ff // (per * CHUNK)
    half = rows // CORES
    chips = dp // CORES
    dma = pltpu.SemaphoreType.DMA
    return pl.pallas_call(
        functools.partial(grad_kernel, dp, layers),
        out_shape=(
            jax.ShapeDtypeStruct((total * rows, CHUNK), BF16),
            jax.ShapeDtypeStruct((dp, 8, 128), F32),
        ),
        in_specs=[pl.BlockSpec(memory_space=pl.ANY)] * 5,
        out_specs=(pl.BlockSpec(memory_space=pl.ANY), pl.BlockSpec(memory_space=pltpu.VMEM)),
        scratch_shapes=[
            pltpu.VMEM((tokens, d), BF16),
            pltpu.VMEM((tokens, d), BF16),
            pltpu.VMEM((tokens, d), BF16),
            pltpu.VMEM((tokens, d), BF16),
            pltpu.VMEM((d, tokens), BF16),
            pltpu.VMEM((d, tokens), BF16),
            pltpu.VMEM((tokens, d), F32),
            pltpu.VMEM((FTILE, ff), BF16),
            pltpu.VMEM((tokens, CHUNK), BF16),
            pltpu.VMEM((tokens, 2 * CHUNK), BF16),
            pltpu.VMEM((layers, per, d, 2 * CHUNK), BF16),
            pltpu.VMEM((layers, ff, d), BF16),
            pltpu.VMEM((TERMS, rows, CHUNK), BF16),
            pltpu.VMEM((HALVES, half, CHUNK), BF16),
            pltpu.VMEM((RUNS, chips, 2, half // chips // 2, CHUNK), BF16),
            pltpu.VMEM((total, rows, CHUNK), BF16),
            pltpu.VMEM((8, 128), F32),
            pltpu.VMEM((dp, 8, 128), F32),
            dma((2,)),
            dma((layers, per, 3)),
            dma((SLOTS,)),
            dma((2, SLOTS)),
            dma((chips - 1, 2, SLOTS)),
            dma((chips - 1, 2, SLOTS)),
            dma((2, total)),
            dma((2, total)),
            dma((2, total)),
            dma((2, total)),
            dma((2, total)),
            dma((dp - 1,)),
            dma((dp - 1,)),
        ],
        compiler_params=pltpu.CompilerParams(collective_id=0, has_side_effects=True, vmem_limit_bytes=67043328),
        name="gradients",
    )(x, dy, wg, wu, wd)


def adamw_kernel(count, ssq, g, *refs):
    ins, outs = refs[:9], refs[9:]
    d = ins[0].shape[1]
    mean = jnp.sum(jnp.sum(ssq[...], 0), keepdims=True) / count
    factor = jnp.minimum(1.0, 0.5 * lax.rsqrt(mean + 1e-30))

    def one(n, index, piece):
        w, m, v = (ins[n + 3 * k] for k in range(3))
        new_w, new_m, new_v = (outs[n + 3 * k] for k in range(3))
        grad = piece.astype(F32) * factor
        wide = w[index].astype(F32)
        m1 = 0.9 * m[index] + 0.1 * grad
        v1 = 0.95 * v[index] + 0.05 * grad * grad
        new_m[index] = m1
        new_v[index] = v1
        new_w[index] = (wide - 0.02 * (m1 * lax.rsqrt(v1 + 1e-8) + 0.1 * wide)).astype(BF16)

    one(0, (0,), g[0:d, :])
    one(1, (0,), g[d : 2 * d, :])
    for n in range(d // CHUNK):
        one(2, (0, slice(None), slice(n * CHUNK, (n + 1) * CHUNK)), g[2 * d + n * CHUNK : 2 * d + (n + 1) * CHUNK, :])


def adamw(ssq, g, weights, m, v):
    layers, d, ff = weights[0].shape
    per = ff // CHUNK
    rows = g.shape[0] // (layers * per)
    wide = pl.BlockSpec((1, d, CHUNK), lambda l, c: (l, 0, c))
    tall = pl.BlockSpec((1, CHUNK, d), lambda l, c: (l, c, 0))
    trio = [wide, wide, tall]
    count = sum(w.size for w in weights)
    return pl.pallas_call(
        functools.partial(adamw_kernel, count),
        grid=(layers, per),
        out_shape=tuple(jax.ShapeDtypeStruct(a.shape, a.dtype) for a in (*weights, *m, *v)),
        in_specs=[
            pl.BlockSpec(ssq.shape, lambda l, c: (0, 0, 0)),
            pl.BlockSpec((rows, CHUNK), lambda l, c: ((layers - 1 - l) * per + c, 0)),
            *trio, *trio, *trio,
        ],
        out_specs=tuple(trio * 3),
        compiler_params=pltpu.CompilerParams(vmem_limit_bytes=48 * 2**20),
        name="adamw",
    )(ssq, g, *weights, *m, *v)


def solution(mesh):
    dp = mesh.shape["dp"]

    def step(x, dy, *arrays):
        weights, m, v = (arrays[i : i + 3] for i in (0, 3, 6))
        g, ssq = gradients(x[0], dy[0], *weights, dp)
        return adamw(ssq, g, weights, m, v)

    return jax.shard_map(
        step,
        mesh=mesh,
        in_specs=(P(("rep", "dp"), None, None),) * 2 + (P(None, None, None),) * 9,
        out_specs=(P("rep", None, None),) * 9,
        check_vma=False,
    )
```

time: 407 us -> 218 us (0.54); the launches traced: 399 us -> 218 us
  Pallas kernels: 0 us -> 214 us
  matrix products: 179 us -> 0 us
  waiting for transfers between devices: 138 us -> 0 us
  other arithmetic: 56.6 us -> 0 us
  between operations: 16.7 us -> 0.82 us
  local copies, waits for them, and re-layouts: 8.48 us -> 2.94 us
    pallas_call x0 -> x2, Pallas kernels: none -> 214 us  [the longest x1 165 us: gradients(): pl.pallas_call(functools.partial(grad_kernel, dp, layers), out_shape=(jax...]
    dot_general x15 -> x0, matrix products: 179 us -> none  [the longest x5 67.3 us: layer(): gate = jnp.dot(a, w['w_gate'], preferred_element_type=jnp.float32)]
    psum x1 -> x0, waiting for transfers between devices: 138 us -> none  [step(): summed[number] = [lax.psum(by_w[name], 'dp') for name in NAMES]]
    convert_element_type x2 -> x0, other arithmetic: 43.2 us -> none  [adamw(): return ((w - 0.02 * step).astype(jnp.bfloat16), m, v)]
    reduce_sum x4 -> x0, other arithmetic: 12 us -> none  [the longest x3 11.5 us: step(): jnp.sum(g * g)]
    unnamed x46 -> x4, local copies, waits for them, and re-layouts: 8.48 us -> 2.94 us
  transfers between devices with their start and end apart: 1 -> 0, of which waited for: 1 -> 0; matrix products, arithmetic and copies ran while one was open for 0% -> 0% of each run, Pallas kernels for 0% -> 0%
where the time goes in v1:
time: 218 us
  Pallas kernels  214 us (98%)
  local copies, waits for them, and re-layouts  2.94 us (1%)
    pallas_call x1, Pallas kernels, gradients(): pl.pallas_call(functools.partial(grad_kernel, dp, layers), out_shape=(jax...  165 us
    pallas_call x1, Pallas kernels, adamw(): pl.pallas_call(functools.partial(adamw_kernel, count), grid=(layers, per)...  48.3 us

profile of v1, /device:TPU:113, one launch (start us, length us, event | category | flops | bytes accessed | tf_op | source)
XLA Modules:
  0.0 217.5 jit_solution(2177461643843356661)
XLA Ops:
  0.6 165.5 %gradients.1 = (bf16[24576,256]{1,0:T(8,128)(2,1)}, f32[8,8,128]{2,1,0:T(8,128)}) custom-call(bf16[2048,512]{1,0:T(8,128)(2,1)} %bitcast.2, bf16[2048,512]{1,0:T(8,128)(2,1)} %bitcast.3, bf16[2,512,2048]{2,1,0:T(8,128)(2,1)} %refs_0_.1, bf16[2,512,2048]{2,1,0:T(8,128)(2,1)} %refs_1_.1, bf16[2,2048,512]{2,1,0:T(8,128)(2,1)} %refs_2_.1), custom_call_target="tpu_custom_call" | custom-call | tf_op jit(solution)/shard_map/gradients/pallas_call | solution.py:312
  166.1 0.0 copy-start
  166.2 2.2 %copy-done = bf16[2,512,2048]{2,1,0:T(8,128)(2,1)S(1)} copy-done((bf16[2,512,2048]{2,1,0:T(8,128)(2,1)S(1)}, bf16[2,512,2048]{2,1,0:T(8,128)(2,1)}, u32[]{:S(2)}) %copy-start) | copy-done | bytes 4194328
  168.3 0.0 copy-start.1
  168.3 0.8 copy-done.1
  169.1 48.3 %adamw.1 = (bf16[2,512,2048]{2,1,0:T(8,128)(2,1)}, bf16[2,512,2048]{2,1,0:T(8,128)(2,1)}, bf16[2,2048,512]{2,1,0:T(8,128)(2,1)}, f32[2,512,2048]{2,1,0:T(8,128)}...) custom-call(f32[8,8,128]{2,1,0:T(8,128)S(1)} %copy-done.1, ...), custom_call_target="tpu_custom_call" | custom-call | tf_op jit(solution)/shard_map/adamw/pallas_call | solution.py:389
Async XLA Ops:
  166.1 2.2 %copy-start = (bf16[2,512,2048]{2,1,0:T(8,128)(2,1)S(1)}, bf16[2,512,2048]{2,1,0:T(8,128)(2,1)}, u32[]{:S(2)}) copy-start(bf16[2,512,2048]{2,1,0:T(8,128)(2,1)} %refs_0_.1) | copy-start | bytes 12582916
  168.3 0.8 copy-start.1

commit v2 on v1

--- a/solution.py
+++ b/solution.py
@@ -13,10 +13,15 @@
 CHUNK = 256
 TILE = 512
 FTILE = 256
-SLOTS = 4
-TERMS = 5
-HALVES = 7
-RUNS = 6
+LAG = 1
+GATHER_LAG = 2
+STEPS = 4
+SLOTS = 2 * LAG + 2
+TERMS = STEPS * LAG + 1
+HALVES = (STEPS + 1) * LAG + 2
+RUNS = STEPS * LAG + 2
+PART = 8
+LATE = 8
 COMM = True
 
 
@@ -37,15 +42,16 @@
 
 
 def grad_kernel(
-    dp, layers, x_hbm, dy_hbm, wg_hbm, wu_hbm, wd_hbm, g_hbm, ssq_out,
-    xv, dyv, hv, av, at, dt, acc, actf, act, dgu, wgu, wd, term, from_core, run, g, ssq, ssq_all,
-    io_sem, w_sem, out_sem, core_sem, ring_send, ring_recv, near_send, near_recv, far_send, far_recv, half_sem, ssq_send, ssq_recv,
+    dp, layers, x_hbm, dy_hbm, wg_hbm, wu_hbm, wd_hbm, g_hbm, mine_hbm, ssq_out,
+    xv, dyv, hv, av, at, dt, acc, actf, act, dgu, wgu, wd, term, from_core, run, g, mine, ssq, ssq_all,
+    io_sem, w_sem, out_sem, mine_sem, core_sem, ring_send, ring_recv, near_send, near_recv, far_send, far_recv, half_sem, ssq_send, ssq_recv,
 ):
     tokens, d = xv.shape
     ff = wd_hbm.shape[1]
     per = ff // CHUNK
     total = layers * per
     chips = dp // CORES
+    early = total - LATE
     rows = g.shape[1]
     half = rows // CORES
     own = half // chips
@@ -131,11 +137,16 @@
                 acc[at_t, :] += by_a
         slot = i % TERMS
         by_gu = dot(at[...], dgu[...]).astype(BF16)
-        term[slot, 0:d, :] = by_gu[:, :CHUNK]
-        term[slot, d : 2 * d, :] = by_gu[:, CHUNK:]
         by_d = dot(dt[...], act[...]).T.astype(BF16)
-        for n in range(d // CHUNK):
-            term[slot, 2 * d + n * CHUNK : 2 * d + (n + 1) * CHUNK, :] = by_d[:, n * CHUNK : (n + 1) * CHUNK]
+        blocks = rows // piece
+        n, m = d // blocks, CHUNK // blocks
+        for b in range(blocks):
+            start = b * piece
+            term[slot, start : start + n, :] = by_gu[b * n : (b + 1) * n, :CHUNK]
+            term[slot, start + n : start + 2 * n, :] = by_gu[b * n : (b + 1) * n, CHUNK:]
+            for k in range(d // CHUNK):
+                low = start + 2 * n + k * m
+                term[slot, low : low + m, :] = by_d[b * m : (b + 1) * m, k * CHUNK : (k + 1) * CHUNK]
 
     def remote(src, dst, send, recv, to):
         return pltpu.make_async_remote_copy(src_ref=src, dst_ref=dst, send_sem=send, recv_sem=recv, device_id=to, device_id_type=MESH)
@@ -174,7 +185,10 @@
         return remote(place, place, half_sem.at[0, j], half_sem.at[1, j], sibling)
 
     def put_out(j):
-        return pltpu.make_async_copy(g.at[j], g_hbm.at[pl.ds(pl.multiple_of(j * rows, rows), rows)], out_sem.at[j % SLOTS])
+        return pltpu.make_async_copy(g.at[j], g_hbm.at[j], out_sem.at[j % SLOTS])
+
+    def put_mine():
+        return pltpu.make_async_copy(mine, mine_hbm, mine_sem)
 
     def add_up(j, p, direction):
         block = (chip + 2 * chips - p) % chips if direction == 0 else (chip + p) % chips
@@ -187,12 +201,19 @@
         if p < chips:
             run[j % RUNS, p - 1, direction] = value
         else:
-            g[j, here, :] = value
+            @pl.when(j < early)
+            def _():
+                g[j, here, :] = value
+
+            @pl.when(j >= early)
+            def _():
+                mine[jnp.maximum(j - early, 0), direction * piece : (direction + 1) * piece, :] = value
+
         return value
 
     def phases(i):
-        def at_chunk(j, body):
-            pl.when((j >= 0) & (j < total))(functools.partial(body, j))
+        def at_chunk(j, body, end=total):
+            pl.when((j >= 0) & (j < end))(functools.partial(body, j))
 
         def start_swap(j):
             swap(j).start()
@@ -211,8 +232,10 @@
                     wide = jnp.sum((wide * wide).reshape(piece // 8, 8, CHUNK), 0)
                     ssq[...] += sum(wide[:, n : n + 128] for n in range(0, CHUNK, 128))
             if p == chips:
-                near(j, 0).start()
-                near(j, 1).start()
+                @pl.when(j < early)
+                def _():
+                    near(j, 0).start()
+                    near(j, 1).start()
 
         def far_phase(j):
             for direction in range(2):
@@ -233,11 +256,11 @@
 
         at_chunk(i, start_swap)
         for p in range(1, chips + 1):
-            at_chunk(i - p, functools.partial(ring_phase, p))
-        at_chunk(i - chips - 1, far_phase)
-        at_chunk(i - chips - 2, share_phase)
-        at_chunk(i - chips - 3, out_phase)
-        at_chunk(i - chips - 4, lambda j: put_out(j).wait())
+            at_chunk(i - LAG * p, functools.partial(ring_phase, p))
+        at_chunk(i - LAG * chips - GATHER_LAG, far_phase, early)
+        at_chunk(i - LAG * chips - 2 * GATHER_LAG, share_phase, early)
+        at_chunk(i - LAG * chips - 3 * GATHER_LAG, out_phase, early)
+        at_chunk(i - LAG * chips - 3 * GATHER_LAG - 1, lambda j: put_out(j).wait(), early)
 
     acc[...] = jnp.zeros_like(acc)
     ssq[...] = jnp.zeros_like(ssq)
@@ -280,22 +303,21 @@
             peer = (me + dp - k) % dp
             return remote(ssq, ssq_all.at[peer], ssq_send.at[k - 1], ssq_recv.at[k - 1], (rep, peer))
 
-        @pl.loop(total, total + chips + 1)
+        @pl.loop(total, total + LAG * chips)
         def _(i):
             phases(i)
 
         for k in range(1, dp):
             to_peer(k).start()
         ssq_all[me] = ssq[...]
-
-        @pl.loop(total + chips + 1, total + chips + 5)
-        def _(i):
+        put_mine().start()
+        for i in range(total + LAG * chips, early + LAG * chips + 3 * GATHER_LAG + 1):
             phases(i)
-
         for k in range(1, dp):
             to_peer(k).wait_send()
             from_peer(k).wait_recv()
         ssq_out[...] = ssq_all[...]
+        put_mine().wait()
     else:
         ssq_out[...] = jnp.zeros_like(ssq_out)
 
@@ -312,11 +334,12 @@
     return pl.pallas_call(
         functools.partial(grad_kernel, dp, layers),
         out_shape=(
-            jax.ShapeDtypeStruct((total * rows, CHUNK), BF16),
+            jax.ShapeDtypeStruct((total - LATE, rows, CHUNK), BF16),
+            jax.ShapeDtypeStruct((LATE, rows // dp, CHUNK), BF16),
             jax.ShapeDtypeStruct((dp, 8, 128), F32),
         ),
         in_specs=[pl.BlockSpec(memory_space=pl.ANY)] * 5,
-        out_specs=(pl.BlockSpec(memory_space=pl.ANY), pl.BlockSpec(memory_space=pltpu.VMEM)),
+        out_specs=(pl.BlockSpec(memory_space=pl.ANY), pl.BlockSpec(memory_space=pl.ANY), pl.BlockSpec(memory_space=pltpu.VMEM)),
         scratch_shapes=[
             pltpu.VMEM((tokens, d), BF16),
             pltpu.VMEM((tokens, d), BF16),
@@ -333,12 +356,14 @@
             pltpu.VMEM((TERMS, rows, CHUNK), BF16),
             pltpu.VMEM((HALVES, half, CHUNK), BF16),
             pltpu.VMEM((RUNS, chips, 2, half // chips // 2, CHUNK), BF16),
-            pltpu.VMEM((total, rows, CHUNK), BF16),
+            pltpu.VMEM((total - LATE, rows, CHUNK), BF16),
+            pltpu.VMEM((LATE, rows // dp, CHUNK), BF16),
             pltpu.VMEM((8, 128), F32),
             pltpu.VMEM((dp, 8, 128), F32),
             dma((2,)),
             dma((layers, per, 3)),
             dma((SLOTS,)),
+            dma,
             dma((2, SLOTS)),
             dma((chips - 1, 2, SLOTS)),
             dma((chips - 1, 2, SLOTS)),
@@ -355,16 +380,22 @@
     )(x, dy, wg, wu, wd)
 
 
-def adamw_kernel(count, ssq, g, *refs):
-    ins, outs = refs[:9], refs[9:]
-    d = ins[0].shape[1]
+def adamw_kernel(count, n_g, n_old, ids, ssq, *refs):
+    gs, ins, outs = refs[:n_g], refs[n_g : n_g + 9], refs[n_g + 9 + n_old :]
     mean = jnp.sum(jnp.sum(ssq[...], 0), keepdims=True) / count
     factor = jnp.minimum(1.0, 0.5 * lax.rsqrt(mean + 1e-30))
 
-    def one(n, index, piece):
+    def grad(chunk, rows):
+        if n_g == 1:
+            return gs[0][0, chunk, rows, :].astype(F32) * factor
+        value = gs[0][chunk, rows, :]
+        for k in range(1, n_g):
+            value = jnp.where(pl.program_id(0) == k, gs[k][chunk, rows, :], value)
+        return value.astype(F32) * factor
+
+    def one(n, index, grad):
         w, m, v = (ins[n + 3 * k] for k in range(3))
         new_w, new_m, new_v = (outs[n + 3 * k] for k in range(3))
-        grad = piece.astype(F32) * factor
         wide = w[index].astype(F32)
         m1 = 0.9 * m[index] + 0.1 * grad
         v1 = 0.95 * v[index] + 0.05 * grad * grad
@@ -372,42 +403,119 @@
         new_v[index] = v1
         new_w[index] = (wide - 0.02 * (m1 * lax.rsqrt(v1 + 1e-8) + 0.1 * wide)).astype(BF16)
 
-    one(0, (0,), g[0:d, :])
-    one(1, (0,), g[d : 2 * d, :])
-    for n in range(d // CHUNK):
-        one(2, (0, slice(None), slice(n * CHUNK, (n + 1) * CHUNK)), g[2 * d + n * CHUNK : 2 * d + (n + 1) * CHUNK, :])
-
-
-def adamw(ssq, g, weights, m, v):
-    layers, d, ff = weights[0].shape
-    per = ff // CHUNK
-    rows = g.shape[0] // (layers * per)
-    wide = pl.BlockSpec((1, d, CHUNK), lambda l, c: (l, 0, c))
-    tall = pl.BlockSpec((1, CHUNK, d), lambda l, c: (l, c, 0))
+    wide_rows, d = ins[0].shape[1] // 2, ins[2].shape[4]
+    tall_rows = ins[2].shape[3] // 2
+    for chunk in range(PART):
+        for direction in range(2):
+            start = direction * (2 * wide_rows + d // CHUNK * tall_rows)
+            there = (0, slice(direction * wide_rows, (direction + 1) * wide_rows), slice(chunk * CHUNK, (chunk + 1) * CHUNK))
+            one(0, there, grad(chunk, slice(start, start + wide_rows)))
+            one(1, there, grad(chunk, slice(start + wide_rows, start + 2 * wide_rows)))
+            for k in range(d // CHUNK):
+                low = start + 2 * wide_rows + k * tall_rows
+                there = (0, 0, chunk, slice(direction * tall_rows, (direction + 1) * tall_rows), slice(k * CHUNK, (k + 1) * CHUNK))
+                one(2, there, grad(chunk, slice(low, low + tall_rows)))
+
+
+def adamw(dp, count, ids, ssq, gs, arrays, first_part, order, first_id=0, old=None):
+    layers, d, ff = arrays[0].shape
+    per = ff // CHUNK // PART
+
+    def layer(p):
+        return layers - 1 - p // per
+
+    if len(gs) == 1:
+        grid = (dp,)
+
+        def place(i, ids):
+            return first_part, i
+
+        g_specs = [pl.BlockSpec((1, PART, gs[0].shape[2] // dp, CHUNK), lambda i, ids: (first_part, 0, i, 0))]
+    else:
+        grid = (len(gs),)
+
+        def place(i, ids):
+            return first_part, ids[first_id + i]
+
+        g_specs = [pl.BlockSpec(g.shape, lambda i, ids: (0, 0, 0)) for g in gs]
+
+    def wide_index(i, ids):
+        p, s = place(i, ids)
+        return layer(p), s, p % per
+
+    def tall_index(i, ids):
+        p, s = place(i, ids)
+        return layer(p), p % per, 0, s, 0
+
+    wide = pl.BlockSpec((1, d // dp, PART * CHUNK), wide_index)
+    tall = pl.BlockSpec((1, 1, PART, CHUNK // dp, d), tall_index)
     trio = [wide, wide, tall]
-    count = sum(w.size for w in weights)
+    old = old or ()
+    first_old = 2 + len(gs) + 9
+    elements = grid[0] * PART * 3 * d * CHUNK // dp
     return pl.pallas_call(
-        functools.partial(adamw_kernel, count),
-        grid=(layers, per),
-        out_shape=tuple(jax.ShapeDtypeStruct(a.shape, a.dtype) for a in (*weights, *m, *v)),
-        in_specs=[
-            pl.BlockSpec(ssq.shape, lambda l, c: (0, 0, 0)),
-            pl.BlockSpec((rows, CHUNK), lambda l, c: ((layers - 1 - l) * per + c, 0)),
-            *trio, *trio, *trio,
-        ],
-        out_specs=tuple(trio * 3),
-        compiler_params=pltpu.CompilerParams(vmem_limit_bytes=48 * 2**20),
-        name="adamw",
-    )(ssq, g, *weights, *m, *v)
+        functools.partial(adamw_kernel, count, len(gs), len(old)),
+        out_shape=tuple(jax.ShapeDtypeStruct(a.shape, a.dtype) for a in arrays),
+        grid_spec=pltpu.PrefetchScalarGridSpec(
+            num_scalar_prefetch=1,
+            grid=grid,
+            in_specs=[
+                pl.BlockSpec(ssq.shape, lambda i, ids: (0, 0, 0)),
+                *g_specs, *trio, *trio, *trio,
+                *[pl.BlockSpec(memory_space=pl.ANY)] * len(old),
+            ],
+            out_specs=tuple(trio * 3),
+        ),
+        input_output_aliases={first_old + n: n for n in range(len(old))},
+        compiler_params=pltpu.CompilerParams(vmem_limit_bytes=60 * 2**20),
+        cost_estimate=pl.CostEstimate(flops=elements * 40, bytes_accessed=elements * 22, transcendentals=elements),
+        name=f"adamw{order}",
+    )(ids, ssq, *gs, *arrays, *old)
 
 
 def solution(mesh):
     dp = mesh.shape["dp"]
+    chips = dp // CORES
 
     def step(x, dy, *arrays):
-        weights, m, v = (arrays[i : i + 3] for i in (0, 3, 6))
-        g, ssq = gradients(x[0], dy[0], *weights, dp)
-        return adamw(ssq, g, weights, m, v)
+        weights = arrays[:3]
+        layers, d, ff = weights[0].shape
+        count = sum(w.size for w in weights)
+        me = lax.axis_index("dp")
+        chip, core = me // CORES, me % CORES
+        turn = 1 - 2 * core
+        behind, ahead, far = ((chip + chips + n) % chips for n in (-turn, turn, chips // 2))
+        ids = jnp.stack([k * chips + c for k, c in (
+            (core, chip), (1 - core, chip), (core, behind), (core, ahead),
+            (1 - core, ahead), (1 - core, behind), (core, far), (1 - core, far),
+        )])
+
+        def index(chip, core):
+            return chip % chips * CORES + core
+
+        devices = [(c, k) for c in range(chips) for k in range(CORES)]
+        on = [(index(c, k), index(c + 1 - 2 * k, k)) for c, k in devices]
+        back = [(b, a) for a, b in on]
+        over = [(index(c, k), index(c, 1 - k)) for c, k in devices]
+        on_over = [(index(c, k), index(c + 1 - 2 * k, 1 - k)) for c, k in devices]
+
+        g, mine, ssq = gradients(x[0], dy[0], *weights, dp)
+        arrays = [a.reshape(layers, -1, PART, CHUNK, d) if n % 3 == 2 else a for n, a in enumerate(arrays)]
+        g = g.reshape(-1, PART, *g.shape[1:])
+        update = functools.partial(adamw, dp, count, ids, ssq)
+        mine_over = lax.ppermute(mine, "dp", over)
+        one = lax.ppermute(mine, "dp", on)
+        two = lax.ppermute(mine, "dp", back)
+        new = update([g], arrays, 0, 0)
+        one, two, mine_over, new = lax.optimization_barrier((one, two, mine_over, new))
+        far = lax.ppermute(one, "dp", on)
+        far_over = lax.ppermute(one, "dp", on_over)
+        one_over = lax.ppermute(one, "dp", over)
+        two_over = lax.ppermute(two, "dp", over)
+        new = update([mine, mine_over, one, two], arrays, 1, 1, 0, new)
+        one_over, two_over, far, far_over, new = lax.optimization_barrier((one_over, two_over, far, far_over, new))
+        new = update([one_over, two_over, far, far_over], arrays, 1, 2, 4, new)
+        return tuple(a.reshape(layers, ff, d) if n % 3 == 2 else a for n, a in enumerate(new))
 
     return jax.shard_map(
         step,

time: 218 us -> 209 us (0.959)
  Pallas kernels: 214 us -> 198 us
  starting transfers between devices: 0 us -> 5.18 us
  waiting for transfers between devices: 0 us -> 3.88 us
  local copies, waits for them, and re-layouts: 2.94 us -> 0.63 us
    pallas_call x1, Pallas kernels: 165 us -> 144 us  [gradients(): pl.pallas_call(functools.partial(grad_kernel, dp, layers), out_shape=(jax...]
    pallas_call x1 -> x3, Pallas kernels: 48.3 us -> 53.9 us  [adamw(): pl.pallas_call(functools.partial(adamw_kernel, count, len(gs), len(old)),...]
    ppermute x0 -> x7, starting transfers between devices: none -> 5.18 us  [the longest x1 2.26 us: step(): one = lax.ppermute(mine, 'dp', on)]
    ppermute x0 -> x7, waiting for transfers between devices: none -> 3.88 us  [the longest x1 3.86 us: step(): far = lax.ppermute(one, 'dp', on)]
    unnamed x4 -> x8, local copies, waits for them, and re-layouts: 2.94 us -> 0.02 us
  transfers between devices with their start and end apart: 0 -> 7, of which waited for: 0 -> 1; matrix products, arithmetic and copies ran while one was open for 0% -> 0% of each run, Pallas kernels for 0% -> 19%
where the time goes in v2:
time: 209 us; the launch traced here: 208 us
  Pallas kernels  198 us (95%)
  starting transfers between devices  5.18 us (2%)
  waiting for transfers between devices  3.88 us (2%)
    pallas_call x1, Pallas kernels, gradients(): pl.pallas_call(functools.partial(grad_kernel, dp, layers), out_shape=(jax...  144 us
    pallas_call x3, Pallas kernels, adamw(): pl.pallas_call(functools.partial(adamw_kernel, count, len(gs), len(old)),...  53.9 us
  transfers between devices with their start and end apart: 7, of which 1 were waited for; matrix products, arithmetic and copies ran while one was open for 0% of the time, Pallas kernels for 19%

profile of v2, /device:TPU:113, one launch (start us, length us, event | category | flops | bytes accessed | tf_op | source)
XLA Modules:
  0.0 208.3 jit_solution(3038362985227117078)
XLA Ops:
  0.6 143.8 %gradients.1 = (bf16[8,1536,256]{2,1,0:T(8,128)(2,1)}, bf16[8,192,256]{2,1,0:T(8,128)(2,1)}, f32[8,8,128]{2,1,0:T(8,128)}) custom-call(bf16[2048,512]{1,0:T(8,128)(2,1)} %bitcast.30, bf16[2048,512]{1,0:T(8,128)(2,1)} %bitcast.31, bf16[2,512,2048]{2,1,0:T(8,128)(2,1)} %refs_4_.5, bf16[2,512,2048]{2,1,0:T(8,128)(2,1)} %refs_5_.5, bf16[2,2048,512]{2,1,0:T(8,128)(2,1)} %wd_hbm.1), custom_call_target="tpu_custom_call" | custom-call | tf_op jit(solution)/shard_map/gradients/pallas_call | solution.py:334
  144.5 0.5 collective-permute-start.2
  145.0 0.4 collective-permute-start.1
  145.4 2.3 %collective-permute-start = (bf16[8,192,256]{2,1,0:T(8,128)(2,1)}, bf16[8,192,256]{2,1,0:T(8,128)(2,1)S(1)}, u32[]{:S(2)}, u32[]{:S(2)}) collective-permute-start(bf16[8,192,256]{2,1,0:T(8,128)(2,1)} %get-tuple-element.65.refs_0_), channel_id=1, source_target_pairs={{0,2},{1,7},{2,4},{3,1},{4,6},{5,3},{6,0},{7,5},{8,10},{9,15},{10,... | collective-permute-start | bytes 2359304 | tf_op jit(solution)/shard_map/ppermute | solution.py:507
  147.6 0.6 stack.35.ids
  148.2 25.6 %adamw0.1 = (bf16[2,512,2048]{2,1,0:T(8,128)(2,1)}, bf16[2,512,2048]{2,1,0:T(8,128)(2,1)}, bf16[2,1,8,256,512]{4,3,2,1,0:T(8,128)(2,1)}, f32[2,512,2048]{2,1,0:T...) custom-call(s32[8]{0:T(128)} %stack.35.ids, ...), custom_call_target="tpu_custom_call" | custom-call | flops 125829120 | bytes 69206016 | tf_op jit(solution)/shard_map/adamw0/pallas_call | solution.py:456
  173.9 0.0 collective-permute-done.2.refs_1_
  173.9 0.0 copy-start.2
  173.9 0.0 collective-permute-done.1.refs_3_
  173.9 0.0 copy-start.1
  173.9 0.0 collective-permute-done.refs_2_
  173.9 0.0 copy-start
  173.9 0.1 collective-permute-start.4
  174.0 1.9 collective-permute-start.6
  175.9 0.0 collective-permute-start.5
  176.0 0.0 collective-permute-start.3
  176.0 0.0 copy-done.2
  176.0 0.0 copy-done
  176.0 14.2 %adamw1.1 = (bf16[2,512,2048]{2,1,0:T(8,128)(2,1)}, bf16[2,512,2048]{2,1,0:T(8,128)(2,1)}, bf16[2,1,8,256,512]{4,3,2,1,0:T(8,128)(2,1)}, f32[2,512,2048]{2,1,0:T...) custom-call(s32[8]{0:T(128)} %stack.35.ids, ...), custom_call_target="tpu_custom_call", output_to_operand_aliasing={{0}: (15, {}), {1}: (16, {}), {2}: (17, {}), {3}: (18, {}),... | custom-call | flops 62914560 | bytes 34603008 | tf_op jit(solution)/shard_map/adamw1/pallas_call | solution.py:456
  190.2 0.0 collective-permute-done.4.refs_1_
  190.2 0.0 collective-permute-done.6.refs_3_
  190.2 3.9 %collective-permute-done.5.refs_2_ = bf16[8,192,256]{2,1,0:T(8,128)(2,1)} collective-permute-done((bf16[8,192,256]{2,1,0:T(8,128)(2,1)S(1)}, bf16[8,192,256]{2,1,0:T(8,128)(2,1)}, u32[]{:S(2)}, u32[]{:S(2)}) %collective-permute-start.5) | collective-permute-done | bytes 786464 | tf_op jit(solution)/shard_map/ppermute | solution.py:511
  194.1 0.0 collective-permute-done.3.refs_0_
  194.1 14.1 %adamw2.1 = (bf16[2,512,2048]{2,1,0:T(8,128)(2,1)}, bf16[2,512,2048]{2,1,0:T(8,128)(2,1)}, bf16[2,1,8,256,512]{4,3,2,1,0:T(8,128)(2,1)}, f32[2,512,2048]{2,1,0:T...) custom-call(s32[8]{0:T(128)} %stack.35.ids, ...), custom_call_target="tpu_custom_call", output_to_operand_aliasing={{0}: (15, {}), {1}: (16, {}), {2}: (17, {}), {3}: (18, {}),... | custom-call | flops 62914560 | bytes 34603008 | tf_op jit(solution)/shard_map/adamw2/pallas_call | solution.py:456
  (3 shorter events, 0.0 us)
Async XLA Ops:
  144.5 29.4 %collective-permute-start.2 = (bf16[8,192,256]{2,1,0:T(8,128)(2,1)}, bf16[8,192,256]{2,1,0:T(8,128)(2,1)S(1)}, u32[]{:S(2)}, u32[]{:S(2)}) collective-permute-start(bf16[8,192,256]{2,1,0:T(8,128)(2,1)} %get-tuple-element.65.refs_0_), channel_id=1, source_target_pairs={{0,1},{1,0},{2,3},{3,2},{4,5},{5,4},{6,7},{7,6},{8,9},{9,8},{10,11... | collective-permute-start | bytes 2359304 | tf_op jit(solution)/shard_map/ppermute | solution.py:506
  145.0 28.9 %collective-permute-start.1 = (bf16[8,192,256]{2,1,0:T(8,128)(2,1)}, bf16[8,192,256]{2,1,0:T(8,128)(2,1)S(1)}, u32[]{:S(2)}, u32[]{:S(2)}) collective-permute-start(bf16[8,192,256]{2,1,0:T(8,128)(2,1)} %get-tuple-element.65.refs_0_), channel_id=1, source_target_pairs={{2,0},{7,1},{4,2},{1,3},{6,4},{3,5},{0,6},{5,7},{10,8},{15,9},{12,... | collective-permute-start | bytes 2359304 | tf_op jit(solution)/shard_map/ppermute | solution.py:508
  145.4 28.5 %collective-permute-start = (bf16[8,192,256]{2,1,0:T(8,128)(2,1)}, bf16[8,192,256]{2,1,0:T(8,128)(2,1)S(1)}, u32[]{:S(2)}, u32[]{:S(2)}) collective-permute-start(bf16[8,192,256]{2,1,0:T(8,128)(2,1)} %get-tuple-element.65.refs_0_), channel_id=1, source_target_pairs={{0,2},{1,7},{2,4},{3,1},{4,6},{5,3},{6,0},{7,5},{8,10},{9,15},{10,... | collective-permute-start | bytes 2359304 | tf_op jit(solution)/shard_map/ppermute | solution.py:507
  173.9 2.1 %copy-start.2 = (bf16[8,192,256]{2,1,0:T(8,128)(2,1)}, bf16[8,192,256]{2,1,0:T(8,128)(2,1)S(1)}, u32[]{:S(2)}) copy-start(bf16[8,192,256]{2,1,0:T(8,128)(2,1)S(1)} %collective-permute-done.2.refs_1_) | copy-start | bytes 2359300
  173.9 2.1 copy-start.1
  173.9 2.1 copy-start
  173.9 16.2 %collective-permute-start.4 = (bf16[8,192,256]{2,1,0:T(8,128)(2,1)S(1)}, bf16[8,192,256]{2,1,0:T(8,128)(2,1)S(1)}, u32[]{:S(2)}, u32[]{:S(2)}) collective-permute-start(bf16[8,192,256]{2,1,0:T(8,128)(2,1)S(1)} %collective-permute-done.1.refs_3_), channel_id=1, source_target_pairs={{0,1},{1,0},{2,3},{3,2},{4,5},{5,4},{6,7},{7,6},{8,9},{9,8},{10,11... | collective-permute-start | bytes 2359304 | tf_op jit(solution)/shard_map/ppermute | solution.py:514
  174.0 16.2 %collective-permute-start.6 = (bf16[8,192,256]{2,1,0:T(8,128)(2,1)S(1)}, bf16[8,192,256]{2,1,0:T(8,128)(2,1)}, u32[]{:S(2)}, u32[]{:S(2)}) collective-permute-start(bf16[8,192,256]{2,1,0:T(8,128)(2,1)S(1)} %collective-permute-done.refs_2_), channel_id=1, source_target_pairs={{0,3},{1,6},{2,5},{3,0},{4,7},{5,2},{6,1},{7,4},{8,11},{9,14},{10,... | collective-permute-start | bytes 2359304 | tf_op jit(solution)/shard_map/ppermute | solution.py:512
  175.9 18.1 %collective-permute-start.5 = (bf16[8,192,256]{2,1,0:T(8,128)(2,1)S(1)}, bf16[8,192,256]{2,1,0:T(8,128)(2,1)}, u32[]{:S(2)}, u32[]{:S(2)}) collective-permute-start(bf16[8,192,256]{2,1,0:T(8,128)(2,1)S(1)} %collective-permute-done.refs_2_), channel_id=1, source_target_pairs={{0,2},{1,7},{2,4},{3,1},{4,6},{5,3},{6,0},{7,5},{8,10},{9,15},{10,... | collective-permute-start | bytes 2359304 | tf_op jit(solution)/shard_map/ppermute | solution.py:511
  176.0 18.1 %collective-permute-start.3 = (bf16[8,192,256]{2,1,0:T(8,128)(2,1)S(1)}, bf16[8,192,256]{2,1,0:T(8,128)(2,1)}, u32[]{:S(2)}, u32[]{:S(2)}) collective-permute-start(bf16[8,192,256]{2,1,0:T(8,128)(2,1)S(1)} %collective-permute-done.refs_2_), channel_id=1, source_target_pairs={{0,1},{1,0},{2,3},{3,2},{4,5},{5,4},{6,7},{7,6},{8,9},{9,8},{10,11... | collective-permute-start | bytes 2359304 | tf_op jit(solution)/shard_map/ppermute | solution.py:513
  190.2 3.9 %copy-start.3 = (bf16[8,192,256]{2,1,0:T(8,128)(2,1)}, bf16[8,192,256]{2,1,0:T(8,128)(2,1)S(1)}, u32[]{:S(2)}) copy-start(bf16[8,192,256]{2,1,0:T(8,128)(2,1)S(1)} %collective-permute-done.4.refs_1_) | copy-start | bytes 2359300

commit v3 on v2

--- a/solution.py
+++ b/solution.py
@@ -11,16 +11,17 @@
 BF16, F32 = jnp.bfloat16, jnp.float32
 CORES = 2
 CHUNK = 256
-TILE = 512
+TILE = 1024
 FTILE = 256
 LAG = 1
 GATHER_LAG = 2
-STEPS = 4
-SLOTS = 2 * LAG + 2
+STEPS = 3
+SLOTS = STEPS * LAG + 2
 TERMS = STEPS * LAG + 1
 HALVES = (STEPS + 1) * LAG + 2
 RUNS = STEPS * LAG + 2
 PART = 8
+FIRST = 5
 LATE = 8
 COMM = True
 
@@ -43,7 +44,7 @@
 
 def grad_kernel(
     dp, layers, x_hbm, dy_hbm, wg_hbm, wu_hbm, wd_hbm, g_hbm, mine_hbm, ssq_out,
-    xv, dyv, hv, av, at, dt, acc, actf, act, dgu, wgu, wd, term, from_core, run, g, mine, ssq, ssq_all,
+    xv, dyv, hv, av, at, acc, actf, act, by_next, dgu, wgu, wd, term, from_core, leaving, coming, g, mine, ssq, ssq_all,
     io_sem, w_sem, out_sem, mine_sem, core_sem, ring_send, ring_recv, near_send, near_recv, far_send, far_recv, half_sem, ssq_send, ssq_recv,
 ):
     tokens, d = xv.shape
@@ -114,18 +115,21 @@
         a = (wide * norm_scale(wide)).astype(BF16)
         av[at_t, :] = a
         at[:, at_t] = a.T
-        dt[:, at_t] = dyv[at_t, :].T
 
     for copy in load_w(1):
         copy.wait()
 
-    def compute(layer, c, i):
+    def compute(layer, c, i, second):
         w_chunk = wgu[layer, c]
-        d_chunk = wd[layer, pl.ds(pl.multiple_of(c * CHUNK, CHUNK), CHUNK), :]
         for t in range(tokens // TILE):
             at_t = slice(t * TILE, (t + 1) * TILE)
             gu = dot(av[at_t, :], w_chunk)
-            by_act = dot_t(dyv[at_t, :], d_chunk).astype(BF16).astype(F32)
+            if second:
+                by_act = by_next[at_t, :].astype(F32)
+            else:
+                both = dot_t(dyv[at_t, :], wd[layer, pl.ds(pl.multiple_of(c * CHUNK, 2 * CHUNK), 2 * CHUNK), :]).astype(BF16)
+                by_act = both[:, :CHUNK].astype(F32)
+                by_next[at_t, :] = both[:, CHUNK:]
             gate, up = gu[:, :CHUNK], gu[:, CHUNK:]
             s = sigmoid(gate)
             silu = gate * s
@@ -137,7 +141,7 @@
                 acc[at_t, :] += by_a
         slot = i % TERMS
         by_gu = dot(at[...], dgu[...]).astype(BF16)
-        by_d = dot(dt[...], act[...]).T.astype(BF16)
+        by_d = lax.dot_general(act[...], dyv[...], (((0,), (0,)), ((), ())), preferred_element_type=F32).astype(BF16)
         blocks = rows // piece
         n, m = d // blocks, CHUNK // blocks
         for b in range(blocks):
@@ -159,10 +163,9 @@
         there = pl.ds(pl.multiple_of(other * half, half), half)
         return remote(term.at[j % TERMS, there], from_core.at[j % HALVES], core_sem.at[0, j % SLOTS], core_sem.at[1, j % SLOTS], sibling)
 
-    def ring(j, step, direction):
-        src, dst = (run.at[j % RUNS, n, direction] for n in (step - 1, step))
-        sems = (step - 1, direction, j % SLOTS)
-        return remote(src, dst, ring_send.at[sems], ring_recv.at[sems], right if direction == 0 else left)
+    def travel(j, k):
+        src = leaving.at[j % RUNS, k] if k < 4 else coming.at[j % RUNS, k - 4]
+        return remote(src, coming.at[j % RUNS, k], ring_send.at[k, j % SLOTS], ring_recv.at[k, j % SLOTS], right if k % 2 == 0 else left)
 
     def near(j, direction, arriving=False):
         if arriving:
@@ -190,26 +193,14 @@
     def put_mine():
         return pltpu.make_async_copy(mine, mine_hbm, mine_sem)
 
-    def add_up(j, p, direction):
-        block = (chip + 2 * chips - p) % chips if direction == 0 else (chip + p) % chips
+    def add_up(j, turn, direction, arrived=()):
+        block = (chip + turn) % chips
         here = rows_at(core, block, direction)
         within = pl.ds(pl.multiple_of(block * own + direction * piece, piece), piece)
         value = term[j % TERMS, here, :].astype(F32) + from_core[j % HALVES, within, :].astype(F32)
-        if p > 1:
-            value = value + run[j % RUNS, p - 1, direction].astype(F32)
-        value = value.astype(BF16)
-        if p < chips:
-            run[j % RUNS, p - 1, direction] = value
-        else:
-            @pl.when(j < early)
-            def _():
-                g[j, here, :] = value
-
-            @pl.when(j >= early)
-            def _():
-                mine[jnp.maximum(j - early, 0), direction * piece : (direction + 1) * piece, :] = value
-
-        return value
+        for k in arrived:
+            value = value + coming[j % RUNS, k].astype(F32)
+        return value.astype(BF16)
 
     def phases(i):
         def at_chunk(j, body, end=total):
@@ -218,24 +209,44 @@
         def start_swap(j):
             swap(j).start()
 
-        def ring_phase(p, j):
-            if p == 1:
-                swap(j).wait()
+        def through(j):
+            swap(j).wait()
+            for k in range(2):
+                leaving[j % RUNS, k] = add_up(j, chips // 2, k)
+                travel(j, k).start()
+
+        def onward(j):
+            for k in range(2):
+                travel(j, k).wait()
+                coming[j % RUNS, k] = add_up(j, 1 if k == 0 else chips - 1, k, (k,))
+                travel(j, k + 4).start()
+
+        def alone(j):
+            for k in range(2, 4):
+                leaving[j % RUNS, k] = add_up(j, 1 if k == 2 else chips - 1, 3 - k)
+                travel(j, k).start()
+
+        def finish(j):
+            for k in range(2, 6):
+                travel(j, k).wait()
             for direction in range(2):
-                if p > 1:
-                    ring(j, p - 1, direction).wait()
-                value = add_up(j, p, direction)
-                if p < chips:
-                    ring(j, p, direction).start()
-                else:
-                    wide = value.astype(F32)
-                    wide = jnp.sum((wide * wide).reshape(piece // 8, 8, CHUNK), 0)
-                    ssq[...] += sum(wide[:, n : n + 128] for n in range(0, CHUNK, 128))
-            if p == chips:
+                value = add_up(j, 0, direction, (3 - direction, 4 + direction))
+                wide = value.astype(F32)
+                wide = jnp.sum((wide * wide).reshape(piece // 8, 8, CHUNK), 0)
+                ssq[...] += sum(wide[:, n : n + 128] for n in range(0, CHUNK, 128))
+
                 @pl.when(j < early)
                 def _():
-                    near(j, 0).start()
-                    near(j, 1).start()
+                    g[j, rows_at(core, chip, direction), :] = value
+
+                @pl.when(j >= early)
+                def _():
+                    mine[jnp.maximum(j - early, 0), direction * piece : (direction + 1) * piece, :] = value
+
+            @pl.when(j < early)
+            def _():
+                near(j, 0).start()
+                near(j, 1).start()
 
         def far_phase(j):
             for direction in range(2):
@@ -255,23 +266,30 @@
             put_out(j).start()
 
         at_chunk(i, start_swap)
-        for p in range(1, chips + 1):
-            at_chunk(i - LAG * p, functools.partial(ring_phase, p))
-        at_chunk(i - LAG * chips - GATHER_LAG, far_phase, early)
-        at_chunk(i - LAG * chips - 2 * GATHER_LAG, share_phase, early)
-        at_chunk(i - LAG * chips - 3 * GATHER_LAG, out_phase, early)
-        at_chunk(i - LAG * chips - 3 * GATHER_LAG - 1, lambda j: put_out(j).wait(), early)
+        at_chunk(i - LAG, through)
+        at_chunk(i - 2 * LAG, onward)
+        at_chunk(i - LAG, alone)
+        at_chunk(i - 3 * LAG, finish)
+        at_chunk(i - LAG * STEPS - GATHER_LAG, far_phase, early)
+        at_chunk(i - LAG * STEPS - 2 * GATHER_LAG, share_phase, early)
+        at_chunk(i - LAG * STEPS - 3 * GATHER_LAG, out_phase, early)
+        at_chunk(i - LAG * STEPS - 3 * GATHER_LAG - 1, lambda j: put_out(j).wait(), early)
 
     acc[...] = jnp.zeros_like(acc)
     ssq[...] = jnp.zeros_like(ssq)
     if COMM:
         pl.semaphore_wait(barrier, dp - 1)
 
-    @pl.loop(0, per)
-    def _(c):
-        compute(1, c, c)
-        if COMM:
-            phases(c)
+    def run_layer(layer, first):
+        @pl.loop(0, per // 2)
+        def _(pair):
+            for n in range(2):
+                c = 2 * pair + n
+                compute(layer, c, first + c, n == 1)
+                if COMM:
+                    phases(first + c)
+
+    run_layer(1, 0)
 
     @pl.loop(0, tokens // FTILE)
     def _(t):
@@ -282,17 +300,12 @@
         by_h = by_a * scale - wide * (scale * scale * scale * jnp.mean(by_a * wide, -1, keepdims=True))
         by_h = dyv[at_t, :] + by_h.astype(BF16)
         dyv[at_t, :] = by_h
-        dt[:, at_t] = by_h.T
         wide = xv[at_t, :].astype(F32)
         a = (wide * norm_scale(wide)).astype(BF16)
         av[at_t, :] = a
         at[:, at_t] = a.T
 
-    @pl.loop(0, per)
-    def _(c):
-        compute(0, c, c + per)
-        if COMM:
-            phases(c + per)
+    run_layer(0, per)
 
     if COMM:
         def to_peer(k):
@@ -303,7 +316,7 @@
             peer = (me + dp - k) % dp
             return remote(ssq, ssq_all.at[peer], ssq_send.at[k - 1], ssq_recv.at[k - 1], (rep, peer))
 
-        @pl.loop(total, total + LAG * chips)
+        @pl.loop(total, total + LAG * STEPS)
         def _(i):
             phases(i)
 
@@ -311,7 +324,7 @@
             to_peer(k).start()
         ssq_all[me] = ssq[...]
         put_mine().start()
-        for i in range(total + LAG * chips, early + LAG * chips + 3 * GATHER_LAG + 1):
+        for i in range(total + LAG * STEPS, early + LAG * STEPS + 3 * GATHER_LAG + 1):
             phases(i)
         for k in range(1, dp):
             to_peer(k).wait_send()
@@ -346,16 +359,17 @@
             pltpu.VMEM((tokens, d), BF16),
             pltpu.VMEM((tokens, d), BF16),
             pltpu.VMEM((d, tokens), BF16),
-            pltpu.VMEM((d, tokens), BF16),
             pltpu.VMEM((tokens, d), F32),
             pltpu.VMEM((FTILE, ff), BF16),
+            pltpu.VMEM((tokens, CHUNK), BF16),
             pltpu.VMEM((tokens, CHUNK), BF16),
             pltpu.VMEM((tokens, 2 * CHUNK), BF16),
             pltpu.VMEM((layers, per, d, 2 * CHUNK), BF16),
             pltpu.VMEM((layers, ff, d), BF16),
             pltpu.VMEM((TERMS, rows, CHUNK), BF16),
             pltpu.VMEM((HALVES, half, CHUNK), BF16),
-            pltpu.VMEM((RUNS, chips, 2, half // chips // 2, CHUNK), BF16),
+            pltpu.VMEM((RUNS, 4, half // chips // 2, CHUNK), BF16),
+            pltpu.VMEM((RUNS, 6, half // chips // 2, CHUNK), BF16),
             pltpu.VMEM((total - LATE, rows, CHUNK), BF16),
             pltpu.VMEM((LATE, rows // dp, CHUNK), BF16),
             pltpu.VMEM((8, 128), F32),
@@ -365,8 +379,8 @@
             dma((SLOTS,)),
             dma,
             dma((2, SLOTS)),
-            dma((chips - 1, 2, SLOTS)),
-            dma((chips - 1, 2, SLOTS)),
+            dma((6, SLOTS)),
+            dma((6, SLOTS)),
             dma((2, total)),
             dma((2, total)),
             dma((2, total)),
@@ -417,7 +431,7 @@
                 one(2, there, grad(chunk, slice(low, low + tall_rows)))
 
 
-def adamw(dp, count, ids, ssq, gs, arrays, first_part, order, first_id=0, old=None):
+def adamw(dp, count, ids, ssq, gs, arrays, part, order, first, places, old=None):
     layers, d, ff = arrays[0].shape
     per = ff // CHUNK // PART
 
@@ -425,17 +439,15 @@
         return layers - 1 - p // per
 
     if len(gs) == 1:
-        grid = (dp,)
 
         def place(i, ids):
-            return first_part, i
-
-        g_specs = [pl.BlockSpec((1, PART, gs[0].shape[2] // dp, CHUNK), lambda i, ids: (first_part, 0, i, 0))]
+            return part, first + i
+
+        g_specs = [pl.BlockSpec((1, PART, gs[0].shape[2] // dp, CHUNK), lambda i, ids: (part, 0, first + i, 0))]
     else:
-        grid = (len(gs),)
 
         def place(i, ids):
-            return first_part, ids[first_id + i]
+            return part, ids[first + i]
 
         g_specs = [pl.BlockSpec(g.shape, lambda i, ids: (0, 0, 0)) for g in gs]
 
@@ -452,13 +464,13 @@
     trio = [wide, wide, tall]
     old = old or ()
     first_old = 2 + len(gs) + 9
-    elements = grid[0] * PART * 3 * d * CHUNK // dp
+    elements = places * PART * 3 * d * CHUNK // dp
     return pl.pallas_call(
         functools.partial(adamw_kernel, count, len(gs), len(old)),
         out_shape=tuple(jax.ShapeDtypeStruct(a.shape, a.dtype) for a in arrays),
         grid_spec=pltpu.PrefetchScalarGridSpec(
             num_scalar_prefetch=1,
-            grid=grid,
+            grid=(places,),
             in_specs=[
                 pl.BlockSpec(ssq.shape, lambda i, ids: (0, 0, 0)),
                 *g_specs, *trio, *trio, *trio,
@@ -506,15 +518,18 @@
         mine_over = lax.ppermute(mine, "dp", over)
         one = lax.ppermute(mine, "dp", on)
         two = lax.ppermute(mine, "dp", back)
-        new = update([g], arrays, 0, 0)
+        new = update([g], arrays, 0, 0, 0, FIRST)
         one, two, mine_over, new = lax.optimization_barrier((one, two, mine_over, new))
+        one_over = lax.ppermute(one, "dp", over)
+        two_over = lax.ppermute(two, "dp", over)
         far = lax.ppermute(one, "dp", on)
         far_over = lax.ppermute(one, "dp", on_over)
-        one_over = lax.ppermute(one, "dp", over)
-        two_over = lax.ppermute(two, "dp", over)
-        new = update([mine, mine_over, one, two], arrays, 1, 1, 0, new)
-        one_over, two_over, far, far_over, new = lax.optimization_barrier((one_over, two_over, far, far_over, new))
-        new = update([one_over, two_over, far, far_over], arrays, 1, 2, 4, new)
+        new = update([g], arrays, 0, 1, FIRST, dp - FIRST, new)
+        one_over, two_over, new = lax.optimization_barrier((one_over, two_over, new))
+        near = [mine, mine_over, one, two, one_over, two_over]
+        new = update(near, arrays, 1, 2, 0, len(near), new)
+        far, far_over, new = lax.optimization_barrier((far, far_over, new))
+        new = update([far, far_over], arrays, 1, 3, len(near), 2, new)
         return tuple(a.reshape(layers, ff, d) if n % 3 == 2 else a for n, a in enumerate(new))
 
     return jax.shard_map(

time: 209 us -> 197 us (0.943)
  Pallas kernels: 198 us -> 187 us
  waiting for transfers between devices: 3.88 us -> 0.02 us
    pallas_call x1, Pallas kernels: 144 us -> 128 us  [gradients(): pl.pallas_call(functools.partial(grad_kernel, dp, layers), out_shape=(jax...]
    pallas_call x3 -> x4, Pallas kernels: 53.9 us -> 59 us  [adamw(): pl.pallas_call(functools.partial(adamw_kernel, count, len(gs), len(old)),...]
    ppermute x1, waiting for transfers between devices: 3.86 us -> 0.01 us  [step(): far = lax.ppermute(one, 'dp', on)]
  transfers between devices with their start and end apart: 7 -> 7, of which waited for: 1 -> 0; matrix products, arithmetic and copies ran while one was open for 0% -> 0% of each run, Pallas kernels for 19% -> 26%
where the time goes in v3:
time: 197 us
  Pallas kernels  187 us (95%)
  starting transfers between devices  7.22 us (4%)
    pallas_call x1, Pallas kernels, gradients(): pl.pallas_call(functools.partial(grad_kernel, dp, layers), out_shape=(jax...  128 us
    pallas_call x4, Pallas kernels, adamw(): pl.pallas_call(functools.partial(adamw_kernel, count, len(gs), len(old)),...  59 us
  transfers between devices with their start and end apart: 7, of which 0 were waited for; matrix products, arithmetic and copies ran while one was open for 0% of the time, Pallas kernels for 26%

profile of v3, /device:TPU:113, one launch (start us, length us, event | category | flops | bytes accessed | tf_op | source)
XLA Modules:
  0.0 196.7 jit_solution(15040440688130971453)
XLA Ops:
  0.6 127.9 %gradients.1 = (bf16[8,1536,256]{2,1,0:T(8,128)(2,1)}, bf16[8,192,256]{2,1,0:T(8,128)(2,1)}, f32[8,8,128]{2,1,0:T(8,128)}) custom-call(bf16[2048,512]{1,0:T(8,128)(2,1)} %bitcast.34, bf16[2048,512]{1,0:T(8,128)(2,1)} %bitcast.35, bf16[2,512,2048]{2,1,0:T(8,128)(2,1)} %refs_2_.5, bf16[2,512,2048]{2,1,0:T(8,128)(2,1)} %refs_3_.1, bf16[2,2048,512]{2,1,0:T(8,128)(2,1)} %wd_hbm.1), custom_call_target="tpu_custom_call" | custom-call | tf_op jit(solution)/shard_map/gradients/pallas_call | solution.py:347
  128.6 1.1 collective-permute-start
  129.7 0.5 collective-permute-start.1
  130.1 2.2 %collective-permute-start.2 = (bf16[8,192,256]{2,1,0:T(8,128)(2,1)}, bf16[8,192,256]{2,1,0:T(8,128)(2,1)S(1)}, u32[]{:S(2)}, u32[]{:S(2)}) collective-permute-start(bf16[8,192,256]{2,1,0:T(8,128)(2,1)} %get-tuple-element.83.refs_0_), channel_id=1, source_target_pairs={{0,1},{1,0},{2,3},{3,2},{4,5},{5,4},{6,7},{7,6},{8,9},{9,8},{10,11... | collective-permute-start | bytes 2359304 | tf_op jit(solution)/shard_map/ppermute | solution.py:518
  132.3 0.7 stack.35.ids
  133.0 18.2 %adamw0.1 = (bf16[2,512,2048]{2,1,0:T(8,128)(2,1)}, bf16[2,512,2048]{2,1,0:T(8,128)(2,1)}, bf16[2,1,8,256,512]{4,3,2,1,0:T(8,128)(2,1)}, f32[2,512,2048]{2,1,0:T...) custom-call(s32[8]{0:T(128)} %stack.35.ids, ...), custom_call_target="tpu_custom_call" | custom-call | flops 78643200 | bytes 43253760 | tf_op jit(solution)/shard_map/adamw0/pallas_call | solution.py:468
  151.2 0.0 collective-permute-done.refs_2_
  151.2 0.0 copy-start
  151.2 0.0 collective-permute-done.1.refs_3_
  151.2 0.0 copy-start.1
  151.2 0.0 collective-permute-done.2.refs_1_
  151.2 0.0 copy-start.2
  151.2 0.1 collective-permute-start.5
  151.3 0.5 collective-permute-start.6
  151.8 0.2 collective-permute-start.3
  152.0 2.8 %collective-permute-start.4 = (bf16[8,192,256]{2,1,0:T(8,128)(2,1)S(1)}, bf16[8,192,256]{2,1,0:T(8,128)(2,1)}, u32[]{:S(2)}, u32[]{:S(2)}) collective-permute-start(bf16[8,192,256]{2,1,0:T(8,128)(2,1)S(1)} %collective-permute-done.refs_2_), channel_id=1, source_target_pairs={{0,3},{1,6},{2,5},{3,0},{4,7},{5,2},{6,1},{7,4},{8,11},{9,14},{10,... | collective-permute-start | bytes 2359304 | tf_op jit(solution)/shard_map/ppermute | solution.py:526
  154.8 12.1 %adamw1.1 = (bf16[2,512,2048]{2,1,0:T(8,128)(2,1)}, bf16[2,512,2048]{2,1,0:T(8,128)(2,1)}, bf16[2,1,8,256,512]{4,3,2,1,0:T(8,128)(2,1)}, f32[2,512,2048]{2,1,0:T...) custom-call(s32[8]{0:T(128)} %stack.35.ids, ...), custom_call_target="tpu_custom_call", output_to_operand_aliasing={{0}: (12, {}), {1}: (13, {}), {2}: (14, {}), {3}: (15, {}),... | custom-call | flops 47185920 | bytes 25952256 | tf_op jit(solution)/shard_map/adamw1/pallas_call | solution.py:468
  166.9 0.0 collective-permute-done.5.refs_4_
  166.9 0.0 collective-permute-done.6.refs_5_
  166.9 21.0 %adamw2.1 = (bf16[2,512,2048]{2,1,0:T(8,128)(2,1)}, bf16[2,512,2048]{2,1,0:T(8,128)(2,1)}, bf16[2,1,8,256,512]{4,3,2,1,0:T(8,128)(2,1)}, f32[2,512,2048]{2,1,0:T...) custom-call(s32[8]{0:T(128)} %stack.35.ids, ...), custom_call_target="tpu_custom_call", output_to_operand_aliasing={{0}: (17, {}), {1}: (18, {}), {2}: (19, {}), {3}: (20, {}),... | custom-call | flops 94371840 | bytes 51904512 | tf_op jit(solution)/shard_map/adamw2/pallas_call | solution.py:468
  187.9 0.0 collective-permute-done.3.refs_0_
  187.9 0.0 collective-permute-done.4.refs_1_
  187.9 0.9 copy-done.3
  188.8 7.7 %adamw3.1 = (bf16[2,512,2048]{2,1,0:T(8,128)(2,1)}, bf16[2,512,2048]{2,1,0:T(8,128)(2,1)}, bf16[2,1,8,256,512]{4,3,2,1,0:T(8,128)(2,1)}, f32[2,512,2048]{2,1,0:T...) custom-call(s32[8]{0:T(128)} %stack.35.ids, ...), custom_call_target="tpu_custom_call", output_to_operand_aliasing={{0}: (13, {}), {1}: (14, {}), {2}: (15, {}), {3}: (16, {}),... | custom-call | flops 31457280 | bytes 17301504 | tf_op jit(solution)/shard_map/adamw3/pallas_call | solution.py:468
  (4 shorter events, 0.0 us)
Async XLA Ops:
  128.6 22.6 %collective-permute-start = (bf16[8,192,256]{2,1,0:T(8,128)(2,1)}, bf16[8,192,256]{2,1,0:T(8,128)(2,1)S(1)}, u32[]{:S(2)}, u32[]{:S(2)}) collective-permute-start(bf16[8,192,256]{2,1,0:T(8,128)(2,1)} %get-tuple-element.83.refs_0_), channel_id=1, source_target_pairs={{0,2},{1,7},{2,4},{3,1},{4,6},{5,3},{6,0},{7,5},{8,10},{9,15},{10,... | collective-permute-start | bytes 2359304 | tf_op jit(solution)/shard_map/ppermute | solution.py:519
  129.7 21.5 %collective-permute-start.1 = (bf16[8,192,256]{2,1,0:T(8,128)(2,1)}, bf16[8,192,256]{2,1,0:T(8,128)(2,1)S(1)}, u32[]{:S(2)}, u32[]{:S(2)}) collective-permute-start(bf16[8,192,256]{2,1,0:T(8,128)(2,1)} %get-tuple-element.83.refs_0_), channel_id=1, source_target_pairs={{2,0},{7,1},{4,2},{1,3},{6,4},{3,5},{0,6},{5,7},{10,8},{15,9},{12,... | collective-permute-start | bytes 2359304 | tf_op jit(solution)/shard_map/ppermute | solution.py:520
  130.1 21.1 %collective-permute-start.2 = (bf16[8,192,256]{2,1,0:T(8,128)(2,1)}, bf16[8,192,256]{2,1,0:T(8,128)(2,1)S(1)}, u32[]{:S(2)}, u32[]{:S(2)}) collective-permute-start(bf16[8,192,256]{2,1,0:T(8,128)(2,1)} %get-tuple-element.83.refs_0_), channel_id=1, source_target_pairs={{0,1},{1,0},{2,3},{3,2},{4,5},{5,4},{6,7},{7,6},{8,9},{9,8},{10,11... | collective-permute-start | bytes 2359304 | tf_op jit(solution)/shard_map/ppermute | solution.py:518
  151.2 15.7 %copy-start = (bf16[8,192,256]{2,1,0:T(8,128)(2,1)}, bf16[8,192,256]{2,1,0:T(8,128)(2,1)S(1)}, u32[]{:S(2)}) copy-start(bf16[8,192,256]{2,1,0:T(8,128)(2,1)S(1)} %collective-permute-done.refs_2_) | copy-start | bytes 2359300
  151.2 15.6 %copy-start.1 = (bf16[8,192,256]{2,1,0:T(8,128)(2,1)}, bf16[8,192,256]{2,1,0:T(8,128)(2,1)S(1)}, u32[]{:S(2)}) copy-start(bf16[8,192,256]{2,1,0:T(8,128)(2,1)S(1)} %collective-permute-done.1.refs_3_) | copy-start | bytes 2359300
  151.2 15.6 %copy-start.2 = (bf16[8,192,256]{2,1,0:T(8,128)(2,1)}, bf16[8,192,256]{2,1,0:T(8,128)(2,1)S(1)}, u32[]{:S(2)}) copy-start(bf16[8,192,256]{2,1,0:T(8,128)(2,1)S(1)} %collective-permute-done.2.refs_1_) | copy-start | bytes 2359300
  151.2 15.6 %collective-permute-start.5 = (bf16[8,192,256]{2,1,0:T(8,128)(2,1)S(1)}, bf16[8,192,256]{2,1,0:T(8,128)(2,1)}, u32[]{:S(2)}, u32[]{:S(2)}) collective-permute-start(bf16[8,192,256]{2,1,0:T(8,128)(2,1)S(1)} %collective-permute-done.refs_2_), channel_id=1, source_target_pairs={{0,1},{1,0},{2,3},{3,2},{4,5},{5,4},{6,7},{7,6},{8,9},{9,8},{10,11... | collective-permute-start | bytes 2359304 | tf_op jit(solution)/shard_map/ppermute | solution.py:523
  151.3 15.5 %collective-permute-start.6 = (bf16[8,192,256]{2,1,0:T(8,128)(2,1)S(1)}, bf16[8,192,256]{2,1,0:T(8,128)(2,1)}, u32[]{:S(2)}, u32[]{:S(2)}) collective-permute-start(bf16[8,192,256]{2,1,0:T(8,128)(2,1)S(1)} %collective-permute-done.1.refs_3_), channel_id=1, source_target_pairs={{0,1},{1,0},{2,3},{3,2},{4,5},{5,4},{6,7},{7,6},{8,9},{9,8},{10,11... | collective-permute-start | bytes 2359304 | tf_op jit(solution)/shard_map/ppermute | solution.py:524
  151.8 36.0 %collective-permute-start.3 = (bf16[8,192,256]{2,1,0:T(8,128)(2,1)S(1)}, bf16[8,192,256]{2,1,0:T(8,128)(2,1)S(1)}, u32[]{:S(2)}, u32[]{:S(2)}) collective-permute-start(bf16[8,192,256]{2,1,0:T(8,128)(2,1)S(1)} %collective-permute-done.refs_2_), channel_id=1, source_target_pairs={{0,2},{1,7},{2,4},{3,1},{4,6},{5,3},{6,0},{7,5},{8,10},{9,15},{10,... | collective-permute-start | bytes 2359304 | tf_op jit(solution)/shard_map/ppermute | solution.py:525
  152.0 35.9 %collective-permute-start.4 = (bf16[8,192,256]{2,1,0:T(8,128)(2,1)S(1)}, bf16[8,192,256]{2,1,0:T(8,128)(2,1)}, u32[]{:S(2)}, u32[]{:S(2)}) collective-permute-start(bf16[8,192,256]{2,1,0:T(8,128)(2,1)S(1)} %collective-permute-done.refs_2_), channel_id=1, source_target_pairs={{0,3},{1,6},{2,5},{3,0},{4,7},{5,2},{6,1},{7,4},{8,11},{9,14},{10,... | collective-permute-start | bytes 2359304 | tf_op jit(solution)/shard_map/ppermute | solution.py:526
  187.9 0.9 copy-start.3

commit v4 on v3

--- a/solution.py
+++ b/solution.py
@@ -21,8 +21,6 @@
 HALVES = (STEPS + 1) * LAG + 2
 RUNS = STEPS * LAG + 2
 PART = 8
-FIRST = 5
-LATE = 8
 COMM = True
 
 
@@ -34,6 +32,10 @@
     return lax.dot_general(a, b, (((1,), (1,)), ((), ())), preferred_element_type=F32)
 
 
+def t_dot(a, b):
+    return lax.dot_general(a, b, (((0,), (0,)), ((), ())), preferred_element_type=F32)
+
+
 def sigmoid(z):
     return 0.5 * jnp.tanh(0.5 * z) + 0.5
 
@@ -43,16 +45,15 @@
 
 
 def grad_kernel(
-    dp, layers, x_hbm, dy_hbm, wg_hbm, wu_hbm, wd_hbm, g_hbm, mine_hbm, ssq_out,
-    xv, dyv, hv, av, at, acc, actf, act, by_next, dgu, wgu, wd, term, from_core, leaving, coming, g, mine, ssq, ssq_all,
-    io_sem, w_sem, out_sem, mine_sem, core_sem, ring_send, ring_recv, near_send, near_recv, far_send, far_recv, half_sem, ssq_send, ssq_recv,
+    dp, layers, x_hbm, dy_hbm, wg_hbm, wu_hbm, wd_hbm, g_hbm, behind_hbm, ssq_out,
+    xv, dyv, hv, av, acc, actf, act, by_next, dgu, wgu, wd, term, from_core, leaving, coming, g, ssq, ssq_all,
+    io_sem, w_sem, out_sem, behind_sem, core_sem, ring_send, ring_recv, near_send, near_recv, share_send, share_recv, ssq_send, ssq_recv,
 ):
     tokens, d = xv.shape
     ff = wd_hbm.shape[1]
     per = ff // CHUNK
     total = layers * per
     chips = dp // CORES
-    early = total - LATE
     rows = g.shape[1]
     half = rows // CORES
     own = half // chips
@@ -96,26 +97,31 @@
         copy.start()
 
     load_x().wait()
-    for copy in load_w(0):
-        copy.wait()
-    load_dy().wait()
-
-    @pl.loop(0, tokens // FTILE)
-    def _(t):
-        at_t = pl.ds(pl.multiple_of(t * FTILE, FTILE), FTILE)
+    first_w = load_w(0)
+
+    def forward(at_t, arriving):
         wide = xv[at_t, :].astype(F32)
         a = (wide * norm_scale(wide)).astype(BF16)
         for c in range(per):
+            if arriving:
+                for copy in first_w[3 * c : 3 * c + 3]:
+                    copy.wait()
             gu = dot(a, wgu[0, c])
             gate, up = gu[:, :CHUNK], gu[:, CHUNK:]
             actf[:, c * CHUNK : (c + 1) * CHUNK] = (gate * sigmoid(gate) * up).astype(BF16)
         h = xv[at_t, :] + dot(actf[...], wd[0]).astype(BF16)
         hv[at_t, :] = h
         wide = h.astype(F32)
-        a = (wide * norm_scale(wide)).astype(BF16)
-        av[at_t, :] = a
-        at[:, at_t] = a.T
-
+        av[at_t, :] = (wide * norm_scale(wide)).astype(BF16)
+        acc[at_t, :] = jnp.zeros((FTILE, d), F32)
+
+    forward(slice(0, FTILE), True)
+
+    @pl.loop(1, tokens // FTILE)
+    def _(t):
+        forward(pl.ds(pl.multiple_of(t * FTILE, FTILE), FTILE), False)
+
+    load_dy().wait()
     for copy in load_w(1):
         copy.wait()
 
@@ -140,8 +146,8 @@
                 by_a = dot_t(dgu[at_t, :], w_chunk)
                 acc[at_t, :] += by_a
         slot = i % TERMS
-        by_gu = dot(at[...], dgu[...]).astype(BF16)
-        by_d = lax.dot_general(act[...], dyv[...], (((0,), (0,)), ((), ())), preferred_element_type=F32).astype(BF16)
+        by_gu = t_dot(av[...], dgu[...]).astype(BF16)
+        by_d = t_dot(act[...], dyv[...]).astype(BF16)
         blocks = rows // piece
         n, m = d // blocks, CHUNK // blocks
         for b in range(blocks):
@@ -175,23 +181,22 @@
         place = g.at[j, rows_at(core, block, 0, own)]
         return remote(place, place, near_send.at[direction, j], near_recv.at[direction, j], right if direction == 0 else left)
 
-    def far(j, direction, arriving=False):
-        if arriving:
-            block = (chip + 2) % chips
-        else:
-            block = (chip + chips - 1) % chips if direction == 0 else (chip + 1) % chips
-        place = g.at[j, rows_at(core, block, direction)]
-        return remote(place, place, far_send.at[direction, j], far_recv.at[direction, j], right if direction == 0 else left)
-
-    def share(j, arriving=False):
-        place = g.at[j, pl.ds(pl.multiple_of((other if arriving else core) * half, half), half)]
-        return remote(place, place, half_sem.at[0, j], half_sem.at[1, j], sibling)
+    sides = (0, 1, chips - 1)
+
+    def share(j, n, arriving=False):
+        place = g.at[j, rows_at(other if arriving else core, (chip + sides[n]) % chips, 0, own)]
+        return remote(place, place, share_send.at[n, j], share_recv.at[n, j], sibling)
 
     def put_out(j):
-        return pltpu.make_async_copy(g.at[j], g_hbm.at[j], out_sem.at[j % SLOTS])
-
-    def put_mine():
-        return pltpu.make_async_copy(mine, mine_hbm, mine_sem)
+        copies = []
+        for n in range(2 * len(sides)):
+            rows_n = rows_at(n % 2, (chip + sides[n // 2]) % chips, 0, own)
+            copies.append(pltpu.make_async_copy(g.at[j, rows_n], g_hbm.at[j, rows_n], out_sem.at[n, j % SLOTS]))
+        return copies
+
+    def put_behind(j):
+        behind = (chip + chips - 1 + 2 * core) % chips
+        return pltpu.make_async_copy(g.at[j, rows_at(core, behind, 0, own)], behind_hbm.at[j], behind_sem.at[j % SLOTS])
 
     def add_up(j, turn, direction, arrived=()):
         block = (chip + turn) % chips
@@ -235,47 +240,40 @@
                 wide = jnp.sum((wide * wide).reshape(piece // 8, 8, CHUNK), 0)
                 ssq[...] += sum(wide[:, n : n + 128] for n in range(0, CHUNK, 128))
 
-                @pl.when(j < early)
-                def _():
-                    g[j, rows_at(core, chip, direction), :] = value
-
-                @pl.when(j >= early)
-                def _():
-                    mine[jnp.maximum(j - early, 0), direction * piece : (direction + 1) * piece, :] = value
-
-            @pl.when(j < early)
-            def _():
-                near(j, 0).start()
-                near(j, 1).start()
-
-        def far_phase(j):
+                g[j, rows_at(core, chip, direction), :] = value
+            near(j, 0).start()
+            near(j, 1).start()
+            share(j, 0).start()
+
+        def spread(j):
             for direction in range(2):
                 near(j, direction).wait_send()
                 near(j, direction, True).wait_recv()
-                far(j, direction).start()
-
-        def share_phase(j):
-            for direction in range(2):
-                far(j, direction).wait_send()
-                far(j, direction, True).wait_recv()
-            share(j).start()
-
-        def out_phase(j):
-            share(j).wait_send()
-            share(j, True).wait_recv()
-            put_out(j).start()
+            for n in range(1, 3):
+                share(j, n).start()
+            put_behind(j).start()
+
+        def leave(j):
+            for n in range(3):
+                share(j, n).wait_send()
+                share(j, n, True).wait_recv()
+            for copy in put_out(j):
+                copy.start()
+
+        def left_already(j):
+            put_behind(j).wait()
+            for copy in put_out(j):
+                copy.wait()
 
         at_chunk(i, start_swap)
         at_chunk(i - LAG, through)
         at_chunk(i - 2 * LAG, onward)
         at_chunk(i - LAG, alone)
         at_chunk(i - 3 * LAG, finish)
-        at_chunk(i - LAG * STEPS - GATHER_LAG, far_phase, early)
-        at_chunk(i - LAG * STEPS - 2 * GATHER_LAG, share_phase, early)
-        at_chunk(i - LAG * STEPS - 3 * GATHER_LAG, out_phase, early)
-        at_chunk(i - LAG * STEPS - 3 * GATHER_LAG - 1, lambda j: put_out(j).wait(), early)
-
-    acc[...] = jnp.zeros_like(acc)
+        at_chunk(i - STEPS * LAG - GATHER_LAG, spread)
+        at_chunk(i - STEPS * LAG - 2 * GATHER_LAG, leave)
+        at_chunk(i - STEPS * LAG - 2 * GATHER_LAG - 1, left_already)
+
     ssq[...] = jnp.zeros_like(ssq)
     if COMM:
         pl.semaphore_wait(barrier, dp - 1)
@@ -301,9 +299,7 @@
         by_h = dyv[at_t, :] + by_h.astype(BF16)
         dyv[at_t, :] = by_h
         wide = xv[at_t, :].astype(F32)
-        a = (wide * norm_scale(wide)).astype(BF16)
-        av[at_t, :] = a
-        at[:, at_t] = a.T
+        av[at_t, :] = (wide * norm_scale(wide)).astype(BF16)
 
     run_layer(0, per)
 
@@ -323,14 +319,14 @@
         for k in range(1, dp):
             to_peer(k).start()
         ssq_all[me] = ssq[...]
-        put_mine().start()
-        for i in range(total + LAG * STEPS, early + LAG * STEPS + 3 * GATHER_LAG + 1):
+        @pl.loop(total + LAG * STEPS, total + LAG * STEPS + 2 * GATHER_LAG + 1)
+        def _(i):
             phases(i)
+
         for k in range(1, dp):
             to_peer(k).wait_send()
             from_peer(k).wait_recv()
         ssq_out[...] = ssq_all[...]
-        put_mine().wait()
     else:
         ssq_out[...] = jnp.zeros_like(ssq_out)
 
@@ -347,8 +343,8 @@
     return pl.pallas_call(
         functools.partial(grad_kernel, dp, layers),
         out_shape=(
-            jax.ShapeDtypeStruct((total - LATE, rows, CHUNK), BF16),
-            jax.ShapeDtypeStruct((LATE, rows // dp, CHUNK), BF16),
+            jax.ShapeDtypeStruct((total, rows, CHUNK), BF16),
+            jax.ShapeDtypeStruct((total, rows // dp, CHUNK), BF16),
             jax.ShapeDtypeStruct((dp, 8, 128), F32),
         ),
         in_specs=[pl.BlockSpec(memory_space=pl.ANY)] * 5,
@@ -358,7 +354,6 @@
             pltpu.VMEM((tokens, d), BF16),
             pltpu.VMEM((tokens, d), BF16),
             pltpu.VMEM((tokens, d), BF16),
-            pltpu.VMEM((d, tokens), BF16),
             pltpu.VMEM((tokens, d), F32),
             pltpu.VMEM((FTILE, ff), BF16),
             pltpu.VMEM((tokens, CHUNK), BF16),
@@ -370,22 +365,20 @@
             pltpu.VMEM((HALVES, half, CHUNK), BF16),
             pltpu.VMEM((RUNS, 4, half // chips // 2, CHUNK), BF16),
             pltpu.VMEM((RUNS, 6, half // chips // 2, CHUNK), BF16),
-            pltpu.VMEM((total - LATE, rows, CHUNK), BF16),
-            pltpu.VMEM((LATE, rows // dp, CHUNK), BF16),
+            pltpu.VMEM((total, rows, CHUNK), BF16),
             pltpu.VMEM((8, 128), F32),
             pltpu.VMEM((dp, 8, 128), F32),
             dma((2,)),
             dma((layers, per, 3)),
+            dma((6, SLOTS)),
             dma((SLOTS,)),
-            dma,
             dma((2, SLOTS)),
             dma((6, SLOTS)),
             dma((6, SLOTS)),
             dma((2, total)),
             dma((2, total)),
-            dma((2, total)),
-            dma((2, total)),
-            dma((2, total)),
+            dma((3, total)),
+            dma((3, total)),
             dma((dp - 1,)),
             dma((dp - 1,)),
         ],
@@ -400,11 +393,9 @@
     factor = jnp.minimum(1.0, 0.5 * lax.rsqrt(mean + 1e-30))
 
     def grad(chunk, rows):
-        if n_g == 1:
-            return gs[0][0, chunk, rows, :].astype(F32) * factor
-        value = gs[0][chunk, rows, :]
+        value = gs[0][0, chunk, rows, :]
         for k in range(1, n_g):
-            value = jnp.where(pl.program_id(0) == k, gs[k][chunk, rows, :], value)
+            value = jnp.where(pl.program_id(0) % n_g == k, gs[k][0, chunk, rows, :], value)
         return value.astype(F32) * factor
 
     def one(n, index, grad):
@@ -431,25 +422,21 @@
                 one(2, there, grad(chunk, slice(low, low + tall_rows)))
 
 
-def adamw(dp, count, ids, ssq, gs, arrays, part, order, first, places, old=None):
+def adamw(dp, count, ids, ssq, gs, arrays, order, first, places, old=None):
     layers, d, ff = arrays[0].shape
     per = ff // CHUNK // PART
+    parts = layers * per
 
     def layer(p):
         return layers - 1 - p // per
 
+    def place(i, ids):
+        return i // places, ids[first + i % places]
+
     if len(gs) == 1:
-
-        def place(i, ids):
-            return part, first + i
-
-        g_specs = [pl.BlockSpec((1, PART, gs[0].shape[2] // dp, CHUNK), lambda i, ids: (part, 0, first + i, 0))]
+        g_specs = [pl.BlockSpec((1, PART, gs[0].shape[2] // dp, CHUNK), lambda i, ids: (i // places, 0, ids[first + i % places], 0))]
     else:
-
-        def place(i, ids):
-            return part, ids[first + i]
-
-        g_specs = [pl.BlockSpec(g.shape, lambda i, ids: (0, 0, 0)) for g in gs]
+        g_specs = [pl.BlockSpec((1, *g.shape[1:]), lambda i, ids: (i // places, 0, 0, 0)) for g in gs]
 
     def wide_index(i, ids):
         p, s = place(i, ids)
@@ -464,13 +451,13 @@
     trio = [wide, wide, tall]
     old = old or ()
     first_old = 2 + len(gs) + 9
-    elements = places * PART * 3 * d * CHUNK // dp
+    elements = parts * places * PART * 3 * d * CHUNK // dp
     return pl.pallas_call(
         functools.partial(adamw_kernel, count, len(gs), len(old)),
         out_shape=tuple(jax.ShapeDtypeStruct(a.shape, a.dtype) for a in arrays),
         grid_spec=pltpu.PrefetchScalarGridSpec(
             num_scalar_prefetch=1,
-            grid=(places,),
+            grid=(parts * places,),
             in_specs=[
                 pl.BlockSpec(ssq.shape, lambda i, ids: (0, 0, 0)),
                 *g_specs, *trio, *trio, *trio,
@@ -479,7 +466,7 @@
             out_specs=tuple(trio * 3),
         ),
         input_output_aliases={first_old + n: n for n in range(len(old))},
-        compiler_params=pltpu.CompilerParams(vmem_limit_bytes=60 * 2**20),
+        compiler_params=pltpu.CompilerParams(vmem_limit_bytes=67043328),
         cost_estimate=pl.CostEstimate(flops=elements * 40, bytes_accessed=elements * 22, transcendentals=elements),
         name=f"adamw{order}",
     )(ids, ssq, *gs, *arrays, *old)
@@ -507,29 +494,16 @@
 
         devices = [(c, k) for c in range(chips) for k in range(CORES)]
         on = [(index(c, k), index(c + 1 - 2 * k, k)) for c, k in devices]
-        back = [(b, a) for a, b in on]
-        over = [(index(c, k), index(c, 1 - k)) for c, k in devices]
         on_over = [(index(c, k), index(c + 1 - 2 * k, 1 - k)) for c, k in devices]
 
-        g, mine, ssq = gradients(x[0], dy[0], *weights, dp)
+        g, by_behind, ssq = gradients(x[0], dy[0], *weights, dp)
         arrays = [a.reshape(layers, -1, PART, CHUNK, d) if n % 3 == 2 else a for n, a in enumerate(arrays)]
-        g = g.reshape(-1, PART, *g.shape[1:])
-        update = functools.partial(adamw, dp, count, ids, ssq)
-        mine_over = lax.ppermute(mine, "dp", over)
-        one = lax.ppermute(mine, "dp", on)
-        two = lax.ppermute(mine, "dp", back)
-        new = update([g], arrays, 0, 0, 0, FIRST)
-        one, two, mine_over, new = lax.optimization_barrier((one, two, mine_over, new))
-        one_over = lax.ppermute(one, "dp", over)
-        two_over = lax.ppermute(two, "dp", over)
-        far = lax.ppermute(one, "dp", on)
-        far_over = lax.ppermute(one, "dp", on_over)
-        new = update([g], arrays, 0, 1, FIRST, dp - FIRST, new)
-        one_over, two_over, new = lax.optimization_barrier((one_over, two_over, new))
-        near = [mine, mine_over, one, two, one_over, two_over]
-        new = update(near, arrays, 1, 2, 0, len(near), new)
-        far, far_over, new = lax.optimization_barrier((far, far_over, new))
-        new = update([far, far_over], arrays, 1, 3, len(near), 2, new)
+        g, by_behind = (a.reshape(-1, PART, *a.shape[1:]) for a in (g, by_behind))
+        by_far = lax.ppermute(by_behind, "dp", on)
+        by_far_over = lax.ppermute(by_behind, "dp", on_over)
+        new = adamw(dp, count, ids, ssq, [g], arrays, 0, 0, dp - 2)
+        by_far, by_far_over, new = lax.optimization_barrier((by_far, by_far_over, new))
+        new = adamw(dp, count, ids, ssq, [by_far, by_far_over], arrays, 1, dp - 2, 2, new)
         return tuple(a.reshape(layers, ff, d) if n % 3 == 2 else a for n, a in enumerate(new))
 
     return jax.shard_map(

time: 197 us -> 190 us (0.964)
  starting transfers between devices: 7.22 us -> 2.36 us
    pallas_call x4 -> x2, Pallas kernels: 59 us -> 51.8 us  [adamw(): pl.pallas_call(functools.partial(adamw_kernel, count, len(gs), len(old)),...]
    pallas_call x1, Pallas kernels: 128 us -> 134 us  [gradients(): pl.pallas_call(functools.partial(grad_kernel, dp, layers), out_shape=(jax...]
    ppermute x7 -> x2, starting transfers between devices: 7.22 us -> 2.36 us  [the longest x1 2.28 us: step(): by_far_over = lax.ppermute(by_behind, 'dp', on_over)]
  transfers between devices with their start and end apart: 7 -> 2, of which waited for: 0 -> 0; matrix products, arithmetic and copies ran while one was open for 0% -> 0% of each run, Pallas kernels for 26% -> 20%
where the time goes in v4:
time: 190 us
  Pallas kernels  186 us (98%)
  starting transfers between devices  2.36 us (1%)
    pallas_call x1, Pallas kernels, gradients(): pl.pallas_call(functools.partial(grad_kernel, dp, layers), out_shape=(jax...  134 us
    pallas_call x2, Pallas kernels, adamw(): pl.pallas_call(functools.partial(adamw_kernel, count, len(gs), len(old)),...  51.8 us
  transfers between devices with their start and end apart: 2, of which 0 were waited for; matrix products, arithmetic and copies ran while one was open for 0% of the time, Pallas kernels for 20%

profile of v4, /device:TPU:113, one launch (start us, length us, event | category | flops | bytes accessed | tf_op | source)
XLA Modules:
  0.0 189.8 jit_solution(2091270441898725466)
XLA Ops:
  0.6 134.2 %gradients.1 = (bf16[16,1536,256]{2,1,0:T(8,128)(2,1)}, bf16[16,192,256]{2,1,0:T(8,128)(2,1)}, f32[8,8,128]{2,1,0:T(8,128)}) custom-call(bf16[2048,512]{1,0:T(8,128)(2,1)} %bitcast.28, bf16[2048,512]{1,0:T(8,128)(2,1)} %bitcast.29, bf16[2,512,2048]{2,1,0:T(8,128)(2,1)} %refs_2_.3, bf16[2,512,2048]{2,1,0:T(8,128)(2,1)} %refs_3_.1, bf16[2,2048,512]{2,1,0:T(8,128)(2,1)} %wd_hbm.1), custom_call_target="tpu_custom_call" | custom-call | tf_op jit(solution)/shard_map/gradients/pallas_call | solution.py:343
  134.8 2.3 %collective-permute-start.1 = (bf16[2,8,192,256]{3,2,1,0:T(8,128)(2,1)}, bf16[2,8,192,256]{3,2,1,0:T(8,128)(2,1)}, u32[]{:S(2)}, u32[]{:S(2)}) collective-permute-start(bf16[2,8,192,256]{3,2,1,0:T(8,128)(2,1)} %bitcast.30), channel_id=1, source_target_pairs={{0,3},{1,6},{2,5},{3,0},{4,7},{5,2},{6,1},{7,4},{8,11},{9,14},{10,... | collective-permute-start | bytes 4718600 | tf_op jit(solution)/shard_map/ppermute | solution.py:503
  137.1 0.1 collective-permute-start
  137.2 0.7 stack.35.ids
  137.8 37.8 %adamw0.1 = (bf16[2,512,2048]{2,1,0:T(8,128)(2,1)}, bf16[2,512,2048]{2,1,0:T(8,128)(2,1)}, bf16[2,1,8,256,512]{4,3,2,1,0:T(8,128)(2,1)}, f32[2,512,2048]{2,1,0:T...) custom-call(s32[8]{0:T(128)} %stack.35.ids, ...), custom_call_target="tpu_custom_call" | custom-call | flops 188743680 | bytes 103809024 | tf_op jit(solution)/shard_map/adamw0/pallas_call | solution.py:455
  175.6 0.0 collective-permute-done.1.refs_1_
  175.6 0.0 collective-permute-done.refs_0_
  175.6 14.0 %adamw1.1 = (bf16[2,512,2048]{2,1,0:T(8,128)(2,1)}, bf16[2,512,2048]{2,1,0:T(8,128)(2,1)}, bf16[2,1,8,256,512]{4,3,2,1,0:T(8,128)(2,1)}, f32[2,512,2048]{2,1,0:T...) custom-call(s32[8]{0:T(128)} %stack.35.ids, ...), custom_call_target="tpu_custom_call", output_to_operand_aliasing={{0}: (13, {}), {1}: (14, {}), {2}: (15, {}), {3}: (16, {}),... | custom-call | flops 62914560 | bytes 34603008 | tf_op jit(solution)/shard_map/adamw1/pallas_call | solution.py:455
Async XLA Ops:
  134.8 40.8 %collective-permute-start.1 = (bf16[2,8,192,256]{3,2,1,0:T(8,128)(2,1)}, bf16[2,8,192,256]{3,2,1,0:T(8,128)(2,1)}, u32[]{:S(2)}, u32[]{:S(2)}) collective-permute-start(bf16[2,8,192,256]{3,2,1,0:T(8,128)(2,1)} %bitcast.30), channel_id=1, source_target_pairs={{0,3},{1,6},{2,5},{3,0},{4,7},{5,2},{6,1},{7,4},{8,11},{9,14},{10,... | collective-permute-start | bytes 4718600 | tf_op jit(solution)/shard_map/ppermute | solution.py:503
  137.1 38.5 %collective-permute-start = (bf16[2,8,192,256]{3,2,1,0:T(8,128)(2,1)}, bf16[2,8,192,256]{3,2,1,0:T(8,128)(2,1)}, u32[]{:S(2)}, u32[]{:S(2)}) collective-permute-start(bf16[2,8,192,256]{3,2,1,0:T(8,128)(2,1)} %bitcast.31), channel_id=1, source_target_pairs={{0,2},{1,7},{2,4},{3,1},{4,6},{5,3},{6,0},{7,5},{8,10},{9,15},{10,... | collective-permute-start | bytes 4718600 | tf_op jit(solution)/shard_map/ppermute | solution.py:502

commit v5 on v4

--- a/solution.py
+++ b/solution.py
@@ -125,7 +125,7 @@
     for copy in load_w(1):
         copy.wait()
 
-    def compute(layer, c, i, second):
+    def compute(layer, c, i, second, between):
         w_chunk = wgu[layer, c]
         for t in range(tokens // TILE):
             at_t = slice(t * TILE, (t + 1) * TILE)
@@ -145,6 +145,8 @@
             if layer > 0:
                 by_a = dot_t(dgu[at_t, :], w_chunk)
                 acc[at_t, :] += by_a
+            if t == 0:
+                between()
         slot = i % TERMS
         by_gu = t_dot(av[...], dgu[...]).astype(BF16)
         by_d = t_dot(act[...], dyv[...]).astype(BF16)
@@ -211,9 +213,6 @@
         def at_chunk(j, body, end=total):
             pl.when((j >= 0) & (j < end))(functools.partial(body, j))
 
-        def start_swap(j):
-            swap(j).start()
-
         def through(j):
             swap(j).wait()
             for k in range(2):
@@ -265,7 +264,6 @@
             for copy in put_out(j):
                 copy.wait()
 
-        at_chunk(i, start_swap)
         at_chunk(i - LAG, through)
         at_chunk(i - 2 * LAG, onward)
         at_chunk(i - LAG, alone)
@@ -283,9 +281,9 @@
         def _(pair):
             for n in range(2):
                 c = 2 * pair + n
-                compute(layer, c, first + c, n == 1)
+                compute(layer, c, first + c, n == 1, functools.partial(phases, first + c) if COMM else lambda: None)
                 if COMM:
-                    phases(first + c)
+                    swap(first + c).start()
 
     run_layer(1, 0)
 

time: 190 us -> 188 us (0.989)
  no operation moved by 1% of the time
where the time goes in v5:
time: 188 us
  Pallas kernels  185 us (98%)
    pallas_call x1, Pallas kernels, gradients(): pl.pallas_call(functools.partial(grad_kernel, dp, layers), out_shape=(jax...  133 us
    pallas_call x2, Pallas kernels, adamw(): pl.pallas_call(functools.partial(adamw_kernel, count, len(gs), len(old)),...  51.8 us
  transfers between devices with their start and end apart: 2, of which 0 were waited for; matrix products, arithmetic and copies ran while one was open for 0% of the time, Pallas kernels for 20%

profile of v5, /device:TPU:113, one launch (start us, length us, event | category | flops | bytes accessed | tf_op | source)
XLA Modules:
  0.0 188.1 jit_solution(10306532629047801793)
XLA Ops:
  0.6 132.9 %gradients.1 = (bf16[16,1536,256]{2,1,0:T(8,128)(2,1)}, bf16[16,192,256]{2,1,0:T(8,128)(2,1)}, f32[8,8,128]{2,1,0:T(8,128)}) custom-call(bf16[2048,512]{1,0:T(8,128)(2,1)} %bitcast.28, bf16[2048,512]{1,0:T(8,128)(2,1)} %bitcast.29, bf16[2,512,2048]{2,1,0:T(8,128)(2,1)} %refs_2_.3, bf16[2,512,2048]{2,1,0:T(8,128)(2,1)} %refs_3_.1, bf16[2,2048,512]{2,1,0:T(8,128)(2,1)} %wd_hbm.1), custom_call_target="tpu_custom_call" | custom-call | tf_op jit(solution)/shard_map/gradients/pallas_call | solution.py:341
  133.5 1.8 collective-permute-start.1
  135.3 0.1 collective-permute-start
  135.4 0.7 stack.35.ids
  136.0 37.8 %adamw0.1 = (bf16[2,512,2048]{2,1,0:T(8,128)(2,1)}, bf16[2,512,2048]{2,1,0:T(8,128)(2,1)}, bf16[2,1,8,256,512]{4,3,2,1,0:T(8,128)(2,1)}, f32[2,512,2048]{2,1,0:T...) custom-call(s32[8]{0:T(128)} %stack.35.ids, ...), custom_call_target="tpu_custom_call" | custom-call | flops 188743680 | bytes 103809024 | tf_op jit(solution)/shard_map/adamw0/pallas_call | solution.py:453
  173.8 0.0 collective-permute-done.1.refs_1_
  173.8 0.0 collective-permute-done.refs_0_
  173.8 14.0 %adamw1.1 = (bf16[2,512,2048]{2,1,0:T(8,128)(2,1)}, bf16[2,512,2048]{2,1,0:T(8,128)(2,1)}, bf16[2,1,8,256,512]{4,3,2,1,0:T(8,128)(2,1)}, f32[2,512,2048]{2,1,0:T...) custom-call(s32[8]{0:T(128)} %stack.35.ids, ...), custom_call_target="tpu_custom_call", output_to_operand_aliasing={{0}: (13, {}), {1}: (14, {}), {2}: (15, {}), {3}: (16, {}),... | custom-call | flops 62914560 | bytes 34603008 | tf_op jit(solution)/shard_map/adamw1/pallas_call | solution.py:453
Async XLA Ops:
  133.5 40.3 %collective-permute-start.1 = (bf16[2,8,192,256]{3,2,1,0:T(8,128)(2,1)}, bf16[2,8,192,256]{3,2,1,0:T(8,128)(2,1)}, u32[]{:S(2)}, u32[]{:S(2)}) collective-permute-start(bf16[2,8,192,256]{3,2,1,0:T(8,128)(2,1)} %bitcast.30), channel_id=1, source_target_pairs={{0,3},{1,6},{2,5},{3,0},{4,7},{5,2},{6,1},{7,4},{8,11},{9,14},{10,... | collective-permute-start | bytes 4718600 | tf_op jit(solution)/shard_map/ppermute | solution.py:501
  135.3 38.5 %collective-permute-start = (bf16[2,8,192,256]{3,2,1,0:T(8,128)(2,1)}, bf16[2,8,192,256]{3,2,1,0:T(8,128)(2,1)}, u32[]{:S(2)}, u32[]{:S(2)}) collective-permute-start(bf16[2,8,192,256]{3,2,1,0:T(8,128)(2,1)} %bitcast.31), channel_id=1, source_target_pairs={{0,2},{1,7},{2,4},{3,1},{4,6},{5,3},{6,0},{7,5},{8,10},{9,15},{10,... | collective-permute-start | bytes 4718600 | tf_op jit(solution)/shard_map/ppermute | solution.py:500
